TPU v7x, 32 devices: a whole 2x2x4 slice. The times are simulated.
32 devices in a mesh: gx: 4 (over y, x), gy: 2 (over core), gz: 4 (over z).
Axes of the slice: x: 2, y: 2, z: 4, core: 2. Of those that a mesh axis runs over, the one named last changes fastest.
Arguments:
- right_side: float32 [81, 16, 16, 512], P(None, 'gx', 'gy', 'gz'), may hold values from -18 to 18
- cell_coef: float32 [16, 16, 128], P('gx', 'gy', 'gz'), may hold values from 0.5 to 2
- cell_matrix: float32 [81, 81], replicated, may hold values from -2 to 16, as said below
- face_coupling: float32 [3, 81, 81], replicated, may hold values from -0.18 to 0.18
- patch_inverse: bfloat16 [648, 648], replicated, may hold values from -0.01 to 0.1, as said below
Outputs:
- solution: float32 [81, 16, 16, 512], P(None, 'gx', 'gy', 'gz')
- residual: float32 [81, 16, 16, 512], P(None, 'gx', 'gy', 'gz')
Inputs may be any that keep to these rules, and one draw needn't show every extreme that they name: `cell_matrix`: symmetric. `patch_inverse`: symmetric.
All inputs are finite; a program needn't handle non-finite values.
Results may differ from a plain program's by a relative error of at most 0.035.
Values may be sent and summed in bfloat16 or wider, within the bound.
A program may use at most 192 MiB of HBM per device.

v0:
```python
import functools
import jax
import jax.numpy as jnp
from jax import lax
from jax.experimental import pallas as pl
from jax.experimental.pallas import tpu as pltpu
from jax.sharding import PartitionSpec as P

AXES = ("gx", "gy", "gz")
MESH = pl.DeviceIdType.MESH
F32, BF16 = jnp.float32, jnp.bfloat16
LANES = 128


def class_pairs(d):
    bit = 4 >> d
    return [(c, c + bit) for c in range(8) if not c & bit]


def kernel(sizes, dims, start_ref, inverse_ref, w_ref, sol_ref, res_ref,
           R, S2, Sx, scaled, corr, ccorr, Xx, Xy, Xz,
           fx, fxe, fy, fz, fxes, fys, fzs, mxr, mxe, mxs, myr, mys, mzr,
           mxr_s, mxs_s, myr_s, mys_s, mzr_s, p_rows, p_ref, send_sem, recv_sem):
    D, Q, nr, ni, njh = dims
    w = 2 * nr
    A = Q // 16 * 16
    tiles = [(i, jh) for i in range(ni) for jh in range(njh)]
    C = ni * njh * LANES
    half = njh * LANES
    lane = lax.broadcasted_iota(jnp.int32, (D, LANES), 1)
    jlo0 = (lane // nr) % 2 == 0
    piece = lane // w

    me = [lax.axis_index(a) for a in AXES]

    def neighbour(d, step):
        n = sizes[d]
        return {AXES[d]: lax.rem(me[d] + step + n, n)}

    barrier = pltpu.get_barrier_semaphore()
    for d in range(3):
        for step in (1, -1):
            pl.semaphore_signal(barrier, inc=1, device_id=neighbour(d, step), device_id_type=MESH)

    def rows(c):
        return slice(c * D, (c + 1) * D)

    def cols(i, jh):
        t = i * njh + jh
        return slice(t * LANES, (t + 1) * LANES)

    def get(ref, c):
        return {t: ref[c, :, cols(*t)].astype(F32) for t in tiles}

    def roll(x, s):
        s = s % LANES
        return pltpu.roll(x, s, 1) if s else x

    for c in range(0, 8, 2):
        ox, oy = c // 4, c // 2 % 2
        for i, jh in tiles:
            a = start_ref[2 * i + ox, 4 * jh + oy]
            b = start_ref[2 * i + ox, 4 * jh + 2 + oy]
            R[c, :, cols(i, jh)] = jnp.where(jlo0, a, roll(b, nr))
            R[c + 1, :, cols(i, jh)] = jnp.where(jlo0, roll(a, -nr), b)
    S2[...] = jnp.zeros_like(S2)
    pl.semaphore_wait(barrier, 6)

    def pack_y(ref, last):
        out = []
        for p in class_pairs(1):
            c = p[1] if last else p[0]
            jh = njh - 1 if last else 0
            t0 = ref[c, :, cols(0, jh)].astype(F32)
            t1 = ref[c, :, cols(1, jh)].astype(F32)
            if last:
                out.append(jnp.where(jlo0, roll(t1, -nr), t0))
            else:
                out.append(jnp.where(jlo0, t0, roll(t1, nr)))
        return jnp.stack(out, 0)

    def pack_z(ref, last):
        acc = jnp.zeros((D, LANES), F32)
        n = 0
        for p in class_pairs(2):
            c = p[1] if last else p[0]
            for t in tiles:
                x = ref[c, :, cols(*t)].astype(F32)
                x = roll(x, w * (n + 1) if last else w * n)
                acc = jnp.where(piece == n, x, acc)
                n += 1
        return acc

    def shifted(d, step, have, halo, pc):
        out = {}
        for i, jh in tiles:
            if d == 0:
                at = i + step
                if 0 <= at < ni:
                    new = have[at, jh]
                else:
                    new = halo(slice(jh * LANES, (jh + 1) * LANES))
            elif d == 1:
                at = jh + step
                if 0 <= at < njh:
                    other = roll(have[i, at], step * nr)
                else:
                    other = halo(slice(0, LANES))
                    if i == 0:
                        other = roll(other, step * nr)
                cur = roll(have[i, jh], -step * nr)
                new = jnp.where(jlo0, cur, other) if step == 1 else jnp.where(jlo0, other, cur)
            else:
                n = pc * len(tiles) + i * njh + jh
                h = halo(slice(0, LANES))
                if step == 1:
                    new = jnp.where(lane >= LANES - w, roll(h, LANES - w - w * n),
                                    roll(have[i, jh], -w))
                else:
                    new = jnp.where(lane < w, roll(h, -w * n), roll(have[i, jh], w))
            out[i, jh] = new
        return out

    def read_x(t, last, pc):
        first = lax.broadcasted_iota(jnp.int32, (D - A, LANES), 0) == 0

        def halo(c):
            tail = fxe[t, last, :, c].astype(F32)[pc:pc + 1]
            return jnp.concatenate(
                [fx[t, last, pc, :, c].astype(F32), jnp.where(first, tail, 0.0)], 0)
        return halo

    def read_y(ref, *at):
        return lambda c: ref[(*at, slice(None), c)].astype(F32)

    def remote(src, dst, k, d, step):
        return pltpu.make_async_remote_copy(
            src_ref=src, dst_ref=dst, send_sem=send_sem.at[k], recv_sem=recv_sem.at[k],
            device_id=neighbour(d, step), device_id_type=MESH)

    def move(d, down, copies, halo, beside=None):
        for copy in copies:
            copy.start()
        if beside is not None:
            beside()
        for copy in copies:
            copy.wait()
        for pc, (c0, c1) in enumerate(class_pairs(d)):
            old0, old1 = get(R, c0), get(R, c1)
            if down:
                new0, new1 = shifted(d, -1, old1, halo(pc), pc), old0
            else:
                new0, new1 = old1, shifted(d, 1, old0, halo(pc), pc)
            for t in tiles:
                R[c0, :, cols(*t)] = new0[t]
                R[c1, :, cols(*t)] = new1[t]

    def move_x(down, at, beside=None):
        part = slice((ni - 1) * half, ni * half) if down else slice(0, half)
        cs = slice(4, 8) if down else slice(0, 4)
        mxr_s[...] = R[cs, :A, part].astype(BF16)
        step = 1 if down else -1
        copies = [remote(mxr_s, mxr.at[at], 72 + at, 0, step),
                  remote(R.at[cs, A:A + 8, part], mxe.at[at], 74 + at, 0, step)]
        zeros = jnp.zeros((D - A - 8, LANES), F32)

        def halo(pc):
            return lambda c: jnp.concatenate(
                [mxr[at, pc, :, c].astype(F32), mxe[at, pc, :, c], zeros], 0)
        move(0, down, copies, halo, beside)

    def move_y(down, u):
        myr_s[...] = pack_y(R, down)
        move(1, down, [remote(myr_s, myr.at[u], 64 + u, 1, 1 if down else -1)],
             lambda pc: read_y(myr, u, pc))

    def move_z(down, t):
        mzr_s[...] = pack_z(R, down)
        move(2, down, [remote(mzr_s, mzr.at[t], 48 + t, 2, 1 if down else -1)],
             lambda pc: read_y(mzr, t))

    def sol_y(u):
        return remote(mys_s, mys.at[lax.div(u, 2)], 56 + lax.div(u, 2), 1, -1)

    def sol_x():
        return remote(mxs_s, mxs, 58, 0, -1)

    def pair(ref, q):
        return ref[2 * q:2 * q + 2].reshape(2 * D, C)

    def lessen(q, acc):
        R[2 * q:2 * q + 2] -= acc.reshape(2, D, C)

    def dot(a, b):
        return jnp.dot(a, b, preferred_element_type=F32)

    def colour(t, v, sb):
        for c in range(8):
            s = R[c, Q:Q + 1, :]
            scaled[c] = (s * R[c]).astype(BF16)
        copies = [[None, None] for _ in range(3)]
        extra = [None, None]
        line = lax.broadcasted_iota(jnp.int32, (16, half), 0)
        for n in range(ni):
            part = slice(n * half, (n + 1) * half)
            solved = dot(p_ref[...], scaled[:, :, part].reshape(8 * D, half))
            for c in range(8):
                s = R[c, Q:Q + 1, part]
                k = R[c, Q + 1:Q + 2, part]
                got = s * solved[rows(c), :]
                if v == 1:
                    S2[sb, c, :, part] += got
                corr[c, :, part] = got.astype(BF16)
                ccorr[c, :, part] = (k * got).astype(BF16)
            for last in (0, 1):
                if n != (ni - 1 if last else 0):
                    continue
                step = 1 if last else -1
                tail = jnp.zeros((16, half), F32)
                for pc in range(4):
                    row = corr[4 * last + pc, A:, part].astype(F32)[:1]
                    tail = jnp.where(line == pc, row, tail)
                fxes[last] = tail.astype(BF16)
                copies[0][last] = remote(corr.at[4 * last:4 * last + 4, :A, part], fx.at[t, last],
                                         t * 6 + last, 0, step)
                copies[0][last].start()
                extra[last] = remote(fxes.at[last], fxe.at[t, last], 80 + 2 * t + last, 0, step)
                extra[last].start()
        for last in (0, 1):
            fzs[last] = pack_z(corr, last).astype(BF16)
            copies[2][last] = remote(fzs.at[last], fz.at[t, last], t * 6 + 4 + last, 2, 1 if last else -1)
            copies[2][last].start()
        for last in (0, 1):
            fys[last] = pack_y(corr, last).astype(BF16)
            copies[1][last] = remote(fys.at[last], fy.at[t, last], t * 6 + 2 + last, 1, 1 if last else -1)
            copies[1][last].start()
        for q in range(4):
            acc = dot(w_ref[0], pair(ccorr, q))
            acc += dot(w_ref[1], pair(corr, q))
            acc += dot(w_ref[3 if q // 2 == 0 else 4], pair(corr, q ^ 2))
            acc += dot(w_ref[5 if q % 2 == 0 else 6], pair(corr, q ^ 1))
            lessen(q, acc)

        def fill(d, X, halo0, halo1):
            for pc, (c0, c1) in enumerate(class_pairs(d)):
                new0 = shifted(d, 1, get(corr, c0), halo0(pc), pc)
                new1 = shifted(d, -1, get(corr, c1), halo1(pc), pc)
                for at in tiles:
                    X[c0, :, cols(*at)] = new0[at].astype(BF16)
                    X[c1, :, cols(*at)] = new1[at].astype(BF16)

        for copy in copies[2]:
            copy.wait()
        fill(2, Xz, lambda pc: read_y(fz, t, 0), lambda pc: read_y(fz, t, 1))
        if v == 0:
            for c0, c1 in class_pairs(2):
                S2[sb, c0] += corr[c1].astype(F32)
                S2[sb, c1] += Xz[c0].astype(F32)
        for copy in copies[1]:
            copy.wait()
        fill(1, Xy, lambda pc: read_y(fy, t, 0, pc), lambda pc: read_y(fy, t, 1, pc))
        for q in range(4):
            acc = dot(w_ref[2], pair(Xz, q))
            acc += dot(w_ref[6 if q % 2 == 0 else 5], pair(Xy, q ^ 1))
            lessen(q, acc)
        for copy in copies[0] + extra:
            copy.wait()
        fill(0, Xx, lambda pc: read_x(t, 0, pc), lambda pc: read_x(t, 1, pc))
        for q in range(4):
            lessen(q, dot(w_ref[4 if q // 2 == 0 else 3], pair(Xx, q ^ 2)))

    def class_order():
        r = lax.broadcasted_iota(jnp.int32, (D, 8 * Q), 0)
        k = lax.broadcasted_iota(jnp.int32, (D, 8 * Q), 1)
        for c in range(8):
            pick = jnp.where((k == r * 8 + c) & (r < Q), 1.0, 0.0).astype(BF16)
            p_rows[c * D:(c + 1) * D, :] = dot(pick, inverse_ref[...]).astype(BF16)
        k = lax.broadcasted_iota(jnp.int32, (8 * Q, 8 * D), 0)
        r = lax.broadcasted_iota(jnp.int32, (8 * Q, 8 * D), 1)
        q = r % D
        pick = jnp.where((k == q * 8 + r // D) & (q < Q), 1.0, 0.0).astype(BF16)
        p_ref[...] = dot(p_rows[...], pick).astype(BF16)

    def body(u, carry):
        @pl.when(u == 0)
        def _():
            move_x(True, 0, class_order)

        @pl.when(u == 2)
        def _():
            move_x(False, 1)
            for c in range(8):
                Sx[c] = S2[1, c]
            mxs_s[...] = S2[1, :4, :, :half].astype(BF16)
            sol_x().start()
            S2[1] = jnp.zeros_like(Sx)

        @pl.when(lax.rem(u, 2) == 0)
        def _():
            S2[0] = jnp.zeros_like(Sx)
            move_y(True, u)

        @pl.when(lax.rem(u, 2) == 1)
        def _():
            move_y(False, u)
            mys_s[...] = pack_y(S2.at[0], False).astype(BF16)
            sol_y(u).start()

        for v in (0, 1):
            t = 2 * u + v
            move_z(v == 0, t)
            colour(t, v, lax.rem(u, 2))

        @pl.when(lax.rem(u, 2) == 1)
        def _():
            sol_y(u).wait()
            for pc, (c0, c1) in enumerate(class_pairs(1)):
                S2[1, c0] += S2[0, c1]
                new = shifted(1, 1, get(S2.at[0], c0), read_y(mys, lax.div(u, 2), pc), pc)
                for at in tiles:
                    S2[1, c1, :, cols(*at)] += new[at]
        return carry

    lax.fori_loop(0, 4, body, 0)
    sol_x().wait()
    for pc, (c0, c1) in enumerate(class_pairs(0)):
        S2[1, c0] += Sx[c1]
        new = shifted(0, 1, get(Sx, c0), read_y(mxs, pc), pc)
        for at in tiles:
            S2[1, c1, :, cols(*at)] += new[at]

    for ref, out in ((S2.at[1], sol_ref), (R, res_ref)):
        for c in range(0, 8, 2):
            ox, oy = c // 4, c // 2 % 2
            for i, jh in tiles:
                x0 = ref[c, :, cols(i, jh)]
                x1 = ref[c + 1, :, cols(i, jh)]
                out[2 * i + ox, 4 * jh + oy] = jnp.where(jlo0, x0, roll(x1, nr))
                out[2 * i + ox, 4 * jh + 2 + oy] = jnp.where(jlo0, roll(x0, -nr), x1)


def on_device(sizes, right_side, cell_coef, cell_matrix, face_coupling, patch_inverse):
    Q = cell_matrix.shape[0]
    X, Y, Z = cell_coef.shape
    lanes = right_side.shape[3]
    nr = lanes // Z
    D = -(-(Q + 2) // 16) * 16
    ni, njh = X // 2, Y // 4
    assert lanes == LANES and ni == 2 and 4 * ni * njh * 2 * nr == LANES
    C = ni * njh * LANES
    coef = jnp.repeat(cell_coef, nr, axis=2)
    extra = jnp.stack([lax.rsqrt(coef), coef], 2)
    start = jnp.concatenate(
        [jnp.transpose(right_side, (1, 2, 0, 3)), extra, jnp.zeros((X, Y, D - Q - 2, lanes), F32)], 2)
    def padded(m):
        return jnp.pad(m, ((0, D - Q), (0, D - Q)))

    zero = jnp.zeros((D, D), F32)

    def both(a, b, c, d):
        return jnp.concatenate([jnp.concatenate([a, b], 1), jnp.concatenate([c, d], 1)], 0)

    m = padded(cell_matrix)
    f = [-padded(face_coupling[d]) for d in range(3)]
    ft = [x.T for x in f]
    mats = jnp.stack([
        both(m, zero, zero, m),
        both(zero, f[2], ft[2], zero),
        both(zero, ft[2], f[2], zero),
        both(f[0], zero, zero, f[0]),
        both(ft[0], zero, zero, ft[0]),
        both(f[1], zero, zero, f[1]),
        both(ft[1], zero, zero, ft[1]),
    ]).astype(BF16)
    half = njh * LANES
    V = pltpu.VMEM
    A = Q // 16 * 16
    assert Q == A + 1
    whole = (8, D, C)
    scratch = [
        V(whole, F32), V((2, *whole), F32), V(whole, F32), V(whole, BF16), V(whole, BF16), V(whole, BF16),
        V(whole, BF16), V(whole, BF16), V(whole, BF16),
        V((8, 2, 4, A, half), BF16), V((8, 2, 16, half), BF16),
        V((8, 2, 4, D, LANES), BF16), V((8, 2, D, LANES), BF16),
        V((2, 16, half), BF16), V((2, 4, D, LANES), BF16), V((2, D, LANES), BF16),
        V((2, 4, A, half), BF16), V((2, 4, 8, half), F32), V((4, D, half), BF16),
        V((4, 4, D, LANES), F32), V((2, 4, D, LANES), BF16), V((8, D, LANES), F32),
        V((4, A, half), BF16), V((4, D, half), BF16),
        V((4, D, LANES), F32), V((4, D, LANES), BF16), V((D, LANES), F32),
        V((8 * D, 8 * Q), BF16), V((8 * D, 8 * D), BF16),
        pltpu.SemaphoreType.DMA((96,)), pltpu.SemaphoreType.DMA((96,)),
    ]
    vmem = pl.BlockSpec(memory_space=pltpu.VMEM)
    sol, res = pl.pallas_call(
        functools.partial(kernel, sizes, (D, Q, nr, ni, njh)),
        out_shape=[jax.ShapeDtypeStruct((X, Y, D, lanes), F32)] * 2,
        in_specs=[vmem] * 3,
        out_specs=[vmem] * 2,
        scratch_shapes=scratch,
        compiler_params=pltpu.CompilerParams(
            collective_id=0, has_side_effects=True, vmem_limit_bytes=60 * 1024 * 1024),
    )(start, patch_inverse, mats)
    return tuple(jnp.transpose(x[:, :, :Q], (2, 0, 1, 3)) for x in (sol, res))


def solution(mesh):
    sizes = tuple(mesh.shape[a] for a in AXES)
    placed = (P(None, "gx", "gy", "gz"), P("gx", "gy", "gz"), P(), P(), P())
    return jax.shard_map(
        functools.partial(on_device, sizes),
        mesh=mesh,
        in_specs=placed,
        out_specs=(P(None, "gx", "gy", "gz"), P(None, "gx", "gy", "gz")),
        check_vma=False,
    )
```

profile of v0, /device:TPU:0, one launch (start us, length us, event | category | flops | bytes accessed | tf_op | source)
XLA Modules:
  0.0 155.0 jit_solution(3108383859639493477)
XLA Ops:
  0.6 0.1 pad.62.clone
  0.7 0.8 pad_convert_fusion
  1.5 0.8 copy.31
  2.3 0.8 fusion.32
  3.2 0.1 copy.45
  3.3 0.1 copy.35
  3.4 0.1 copy.46
  3.6 0.1 copy.44
  3.7 0.0 copy-start
  3.7 0.1 fusion.27
  3.8 0.1 copy.39
  3.9 0.1 fusion.29
  4.0 0.1 copy.40
  4.1 0.1 fusion.31
  4.2 0.1 copy.41
  4.3 0.1 copy.34
  4.4 0.1 copy.32
  4.5 0.1 fusion.16
  4.7 0.1 fusion.19
  4.8 0.1 fusion.22
  4.9 0.1 fusion.25.w_ref
  5.0 0.0 copy-done
  5.0 0.0 copy-start.1
  5.0 0.8 copy.48
  5.8 1.5 maximum_maximum_fusion.start_ref
  7.2 0.0 copy-done.1
  7.3 143.1 %shard_map.68 = (f32[4,8,96,128]{3,2,1,0:T(8,128)}, f32[4,8,96,128]{3,2,1,0:T(8,128)}) custom-call(f32[4,8,96,128]{3,2,1,0:T(8,128)} %maximum_maximum_fusion.start_ref, bf16[648,648]{1,0:T(8,128)(2,1)} %inverse_ref.1, bf16[7,192,192]{2,1,0:T(8,128)(2,1)} %copy-done.1), custom_call_target="tpu_custom_call" | custom-call | tf_op jit(solution)/shard_map/pallas_call | solution.py:394
  150.4 2.0 %slice_bitcast_fusion = (f32[81,4,8,128]{3,0,2,1:T(8,128)S(1)}, f32[81,4,8,128]{3,0,2,1:T(8,128)S(1)}) fusion(f32[4,8,96,128]{3,2,1,0:T(8,128)} %get-tuple-element.5, f32[4,8,96,128]{3,2,1,0:T(8,128)} %get-tuple-element.4), kind=kLoop, calls=%fused_computation.2 | loop fusion | bytes 5308416 | tf_op jit(solution)/shard_map/transpose | solution.py:403
  152.4 1.3 copy.43
  153.7 1.3 copy.42
  (12 shorter events, 0.2 us)
Async XLA Ops:
  3.7 1.3 copy-start
  5.0 2.3 %copy-start.1 = (bf16[7,192,192]{2,1,0:T(8,128)(2,1)}, bf16[7,192,192]{2,1,0:T(8,128)(2,1)S(1)}, u32[]{:S(2)}) copy-start(bf16[7,192,192]{2,1,0:T(8,128)(2,1)S(1)} %fusion.25.w_ref) | copy-start | bytes 1548292
where the time goes:
time: 155 us
  Pallas kernels  143 us (92%)
  local copies, waits for them, and re-layouts  8.9 us (6%)
  other arithmetic  2.16 us (1%)
    pallas_call x1, Pallas kernels, on_device(): pl.pallas_call(functools.partial(kernel, sizes, (D, Q, nr, ni, njh)), out...  143 us
    unnamed x14, local copies, waits for them, and re-layouts  4.51 us

commit v1 on v0

--- a/solution.py
+++ b/solution.py
@@ -17,7 +17,7 @@
     return [(c, c + bit) for c in range(8) if not c & bit]
 
 
-def kernel(sizes, dims, start_ref, inverse_ref, w_ref, sol_ref, res_ref,
+def block_kernel(sizes, dims, start_ref, inverse_ref, w_ref, sol_ref, res_ref,
            R, S2, Sx, scaled, corr, ccorr, Xx, Xy, Xz,
            fx, fxe, fy, fz, fxes, fys, fzs, mxr, mxe, mxs, myr, mys, mzr,
            mxr_s, mxs_s, myr_s, mys_s, mzr_s, p_rows, p_ref, send_sem, recv_sem):
@@ -339,7 +339,7 @@
                 out[2 * i + ox, 4 * jh + 2 + oy] = jnp.where(jlo0, roll(x0, -nr), x1)
 
 
-def on_device(sizes, right_side, cell_coef, cell_matrix, face_coupling, patch_inverse):
+def in_blocks(sizes, right_side, cell_coef, cell_matrix, face_coupling, patch_inverse):
     Q = cell_matrix.shape[0]
     X, Y, Z = cell_coef.shape
     lanes = right_side.shape[3]
@@ -392,7 +392,7 @@
     ]
     vmem = pl.BlockSpec(memory_space=pltpu.VMEM)
     sol, res = pl.pallas_call(
-        functools.partial(kernel, sizes, (D, Q, nr, ni, njh)),
+        functools.partial(block_kernel, sizes, (D, Q, nr, ni, njh)),
         out_shape=[jax.ShapeDtypeStruct((X, Y, D, lanes), F32)] * 2,
         in_specs=[vmem] * 3,
         out_specs=[vmem] * 2,
@@ -401,6 +401,536 @@
             collective_id=0, has_side_effects=True, vmem_limit_bytes=60 * 1024 * 1024),
     )(start, patch_inverse, mats)
     return tuple(jnp.transpose(x[:, :, :Q], (2, 0, 1, 3)) for x in (sol, res))
+
+
+def fits_slabs(sizes, Q, X, Y, Z, lanes):
+    group = sizes[0] * sizes[1]
+    layers = Z // group
+    return (lanes == LANES and Q % 16 == 1 and layers == 4 and Z == layers * group
+            and (X // 2) * (Y // 2) == group and lanes // Z == 4 and 2 * layers == group
+            and X % 2 == 0 and Y % 2 == 0)
+
+
+def slab_kernel(sizes, dims, start_ref, coef_ref, inverse_ref, m_ref, f_ref, sol_ref, res_ref,
+                msg, rx, R, S, X, B, W, P, XP, XM, YP, YM, U, p_rows,
+                cr, rr, cr2, rsb, osol, ores, rsol, rres, send_sem, recv_sem):
+    Q, nx, ny, nz, hx, hy = dims
+    G = nx * ny
+    L = 4
+    A = Q - 1
+    T = 4 * A
+    D = T + 16
+    wide = 1
+    while wide * wide < nx:
+        wide += 1
+    lane = lax.broadcasted_iota(jnp.int32, (1, LANES), 1)
+    row16 = lax.broadcasted_iota(jnp.int32, (16, LANES), 0)
+
+    gx, gy, gz = [lax.axis_index(a) for a in AXES]
+    mine = gx * ny + gy
+
+    def snake(p):
+        row = p // wide
+        col = p % wide
+        return row * wide + col + (row % 2) * (wide - 1 - 2 * col)
+
+    def flip(p, plane):
+        return p + (plane % 2) * (nx - 1 - 2 * p)
+
+    slab = flip(snake(gx), gz) * ny + gy
+
+    def device(plane, s):
+        return {"gx": snake(flip(s // ny, plane)), "gy": s % ny, "gz": plane}
+
+    def ring(step):
+        g = lax.rem(gz * G + slab + step + nz * G, nz * G)
+        return device(g // G, g % G)
+
+    def in_plane(o):
+        s = lax.rem(slab + o, G)
+        return s, device(gz, s)
+
+    barrier = pltpu.get_barrier_semaphore()
+    for o in range(1, G):
+        pl.semaphore_signal(barrier, inc=1, device_id=in_plane(o)[1], device_id_type=MESH)
+    for step in (1, -1):
+        pl.semaphore_signal(barrier, inc=1, device_id=ring(step), device_id_type=MESH)
+
+    def remote(src, dst, k, where):
+        return pltpu.make_async_remote_copy(
+            src_ref=src, dst_ref=dst, send_sem=send_sem.at[k], recv_sem=recv_sem.at[k],
+            device_id=where, device_id_type=MESH)
+
+    def roll(x, s):
+        s = s % LANES
+        return pltpu.roll(x, s, 1) if s else x
+
+    def swap(v, index_bit, weight):
+        out = list(v)
+        low = (lane // weight) % 2 == 0
+        for n in range(len(v)):
+            if n & index_bit:
+                continue
+            a, b = v[n], v[n | index_bit]
+            out[n] = jnp.where(low, a, roll(b, weight))
+            out[n | index_bit] = jnp.where(low, roll(a, -weight), b)
+        return out
+
+    bits = [1 << b for b in range(G.bit_length() - 1)]
+    WS = 4 * L
+
+    def swap_slab(v):
+        for b in bits:
+            v = swap(v, b, WS * b)
+        return v
+
+    def swap_source(v):
+        for b in bits:
+            v = swap(v, b, 2 * b)
+        return v
+
+    def lane_x(l):
+        return (l // (2 * ny)) % nx * hx + (l // (WS * hy)) % hx
+
+    def lane_y(l):
+        return (l // 2) % ny * hy + (l // WS) % hy
+
+    def shift_x(v, step):
+        assert hx == 2
+        i0 = (lane // (WS * hy)) % 2
+        g = (lane // (2 * ny)) % nx
+        half, one, all_ = WS * hy, 2 * ny, 2 * ny * (nx - 1)
+        flat = roll(v, half)
+        if step == 1:
+            carry = jnp.where(g < nx - 1, roll(v, half - one), roll(v, half + all_))
+            return jnp.where(i0 == 0, flat, carry)
+        carry = jnp.where(g > 0, roll(v, half + one), roll(v, half - all_))
+        return jnp.where(i0 == 1, flat, carry)
+
+    def shift_y(v, step):
+        assert ny == 2
+        j0 = (lane // WS) % hy
+        g = (lane // 2) % 2
+        back = WS * (hy - 1)
+        if step == 1:
+            carry = jnp.where(g == 0, roll(v, back - 2), roll(v, back + 2))
+            return jnp.where(j0 < hy - 1, roll(v, -WS), carry)
+        carry = jnp.where(g == 0, roll(v, -back - 2), roll(v, -back + 2))
+        return jnp.where(j0 > 0, roll(v, WS), carry)
+
+    def class_rows(q):
+        return slice(q * A, (q + 1) * A)
+
+    cells = [(i, j) for i in range(hx) for j in range(hy)]
+
+    def tail_tile(i, j):
+        out = jnp.zeros((16, LANES), F32)
+        for q in range(4):
+            x, y = 2 * i + q // 2, 2 * j + q % 2
+            k = coef_ref[x, y:y + 1, :]
+            high = k.astype(BF16).astype(F32)
+            out = jnp.where(row16 == q, start_ref[x, y, A:A + 1, :], out)
+            out = jnp.where(row16 == 4 + q, high, out)
+            out = jnp.where(row16 == 8 + q, k - high, out)
+        return out
+
+    for q in range(4):
+        for r in range(0, A, 16):
+            v = swap_slab([start_ref[2 * i + q // 2, 2 * j + q % 2, r:r + 16, :] for i, j in cells])
+            for s in range(G):
+                msg[s, q * A + r:q * A + r + 16, :] = v[s].astype(BF16)
+    v = swap_slab([tail_tile(i, j) for i, j in cells])
+    for s in range(G):
+        msg[s, T:, :] = v[s].astype(BF16)
+    pl.semaphore_wait(barrier, G + 1)
+    arrivals = []
+    for o in range(1, G):
+        s, where = in_plane(o)
+        arrivals.append(remote(msg.at[s], rx.at[mine], 32 + o, where))
+        arrivals[-1].start()
+    rx[mine] = msg[slab]
+
+    def dot(a, b):
+        return jnp.dot(a, b, preferred_element_type=F32)
+
+    def dot_t(a, b):
+        return lax.dot_general(a, b, (((1,), (1,)), ((), ())), preferred_element_type=F32)
+
+    def iota(shape, d):
+        return lax.broadcasted_iota(jnp.int32, shape, d)
+
+    src, dst = iota((2 * LANES, 2 * LANES), 0), iota((2 * LANES, 2 * LANES), 1)
+    same = (src // LANES == dst // LANES) & (src % 2 == dst % 2)
+    sl, dl = src % LANES, dst % LANES
+    for ref, step in ((XP, 1), (XM, hx * nx - 1)):
+        hit = same & (lane_y(sl) == lane_y(dl)) & (lane_x(sl) == (lane_x(dl) + step) % (hx * nx))
+        ref[...] = jnp.where(hit, 1.0, 0.0).astype(BF16)
+    for ref, step in ((YP, 1), (YM, hy * ny - 1)):
+        hit = same & (lane_x(sl) == lane_x(dl)) & (lane_y(sl) == (lane_y(dl) + step) % (hy * ny))
+        ref[...] = jnp.where(hit, 1.0, 0.0).astype(BF16)
+
+    def patch_row(k):
+        d, c = k // 8, k % 8
+        return c % 2 * D + jnp.where(d < A, c // 2 * A + d, T + c // 2)
+
+    pick = patch_row(iota((2 * D, 8 * Q), 1)) == iota((2 * D, 8 * Q), 0)
+    p_rows[...] = dot(jnp.where(pick, 1.0, 0.0).astype(BF16), inverse_ref[...]).astype(BF16)
+    pick = patch_row(iota((8 * Q, 2 * D), 0)) == iota((8 * Q, 2 * D), 1)
+    P[...] = dot(p_rows[...], jnp.where(pick, 1.0, 0.0).astype(BF16)).astype(BF16)
+
+    def packed(k, n):
+        q, d = k // n, k % n
+        return jnp.where(d < A, q * A + d, jnp.where(d == A, T + q, -1))
+
+    def one_hot(hit):
+        return jnp.where(hit, 1.0, 0.0).astype(BF16)
+
+    NR, NC = U.shape[0] // 4, U.shape[1] // 4
+    rows_r = one_hot(packed(iota((D, 4 * NR), 1), NR) == iota((D, 4 * NR), 0))
+    rows_c = one_hot(packed(iota((D, 4 * NC), 1), NC) == iota((D, 4 * NC), 0))
+    cols_r = one_hot(packed(iota((4 * NR, D), 0), NR) == iota((4 * NR, D), 1))
+    cols_c = one_hot(packed(iota((4 * NC, D), 0), NC) == iota((4 * NC, D), 1))
+
+    def table(blocks):
+        U[...] = jnp.zeros_like(U)
+        for a, b, m in blocks:
+            U[a * NR:a * NR + Q, b * NC:b * NC + Q] = m.astype(BF16)
+
+    def plain():
+        return dot(dot(rows_r, U[...]).astype(BF16), cols_c)
+
+    def turned():
+        return dot(dot_t(rows_c, U[...]).astype(BF16), cols_r)
+
+    fx, fy, fz = f_ref[0], f_ref[1], f_ref[2]
+    table([(q, q, -m_ref[...]) for q in range(4)])
+    w = plain().astype(BF16)
+    W[0, :, :D] = w
+    W[1, :, :D] = w
+    table([(0, 2, fx), (1, 3, fx), (0, 1, fy), (2, 3, fy)])
+    w = (plain() + turned()).astype(BF16)
+    W[0, :, D:2 * D] = w
+    W[1, :, D:2 * D] = w
+    table([(2, 0, fx), (3, 1, fx)])
+    w = (plain() + turned()).astype(BF16)
+    W[0, :, 2 * D:3 * D] = w
+    W[1, :, 2 * D:3 * D] = w
+    table([(1, 0, fy), (3, 2, fy)])
+    w = (plain() + turned()).astype(BF16)
+    W[0, :, 3 * D:4 * D] = w
+    W[1, :, 3 * D:4 * D] = w
+    table([(q, q, fz) for q in range(4)])
+    W[0, :, 4 * D:] = plain().astype(BF16)
+    W[1, :, 4 * D:] = turned().astype(BF16)
+    S[...] = jnp.zeros_like(S)
+
+    def z_up(c):
+        return dot(W[0, :, 4 * D:], c)
+
+    def z_down(c):
+        return dot(W[1, :, 4 * D:], c)
+
+    for copy in arrivals:
+        copy.wait()
+    for r in range(0, D, 16):
+        v = swap_source([rx[n, r:r + 16, :].astype(F32) for n in range(G)])
+        for n in range(G):
+            z, h = n // 2, n % 2
+            R[h, z + 1 - h, r:r + 16, :] = v[n]
+
+    def move(ref, h, idx, d, down):
+        shift = shift_x if d == 0 else shift_y
+        bit = 2 >> d
+        for q in range(4):
+            if q & bit:
+                continue
+            old0 = ref[h, idx, class_rows(q), :]
+            old1 = ref[h, idx, class_rows(q + bit), :]
+            if down:
+                ref[h, idx, class_rows(q), :] = shift(old1, -1)
+                ref[h, idx, class_rows(q + bit), :] = old0
+            else:
+                ref[h, idx, class_rows(q), :] = old1
+                ref[h, idx, class_rows(q + bit), :] = shift(old0, 1)
+        t = ref[h, idx, T:, :]
+        upper = (row16 // bit) % 2 == 1
+        if down:
+            t = jnp.where(upper, shift(t, -1), t)
+        else:
+            t = jnp.where(upper, t, shift(t, 1))
+        ref[h, idx, T:, :] = jnp.where(upper, pltpu.roll(t, bit, 0), pltpu.roll(t, 16 - bit, 0))
+
+    copies = []
+    for h in (0, 1):
+        for z in range(L):
+            for d in (0, 1):
+                move(R, h, z + 1 - h, d, True)
+        end, step = (L, 1) if h == 0 else (0, -1)
+        rsb[h] = R[h, end].astype(BF16)
+        copies.append(remote(rsb.at[h], cr2.at[h], 40 + h, ring(step)))
+        copies[-1].start()
+    for h in (0, 1):
+        copies[h].wait()
+        R[h, 0 if h == 0 else L] = cr2[h].astype(F32)
+        for idx in range(L + 1):
+            t = R[h, idx, T:, :]
+            k = t + pltpu.roll(t, 12, 0)
+            k = jnp.where((row16 >= 4) & (row16 < 8), k, 1.0)
+            s = pltpu.roll(lax.rsqrt(k), 4, 0)
+            t = jnp.where(row16 < 4, t, jnp.where(row16 < 8, k, jnp.where(row16 < 12, s, 0.0)))
+            R[h, idx, T:, :] = t
+
+    def split(k):
+        return k % 2, slice(k // 2 * LANES, (k // 2 + 1) * LANES)
+
+    def c_copy(h, base, t, low):
+        z, part = split(0 if low else L - 1)
+        return remote(B.at[h, z, D:2 * D, part], cr.at[t, h], t * 4 + h, ring(-1 if low else 1))
+
+    def r_copy(h, base, t, low):
+        return remote(rsb.at[h], rr.at[t, h], t * 4 + 2 + h, ring(-1 if low else 1))
+
+    def c2_copy(h, low):
+        z, part = split(0 if low else L - 1)
+        return remote(B.at[h, z, D:2 * D, part], cr2.at[h], 42 + h, ring(-1 if low else 1))
+
+    def begin(h, base, t, even, last):
+        low = base == 0
+        first = 0 if low else 1
+        for k in range(L):
+            z, part = split(k)
+            for q in range(4):
+                s = R[h, base + k, T + 8 + q:T + 9 + q, :]
+                X[h, z * D + q * A:z * D + (q + 1) * A, part] = (
+                    R[h, base + k, class_rows(q), :] * s).astype(BF16)
+            t16 = R[h, base + k, T:, :]
+            x16 = jnp.where(row16 < 4, t16 * pltpu.roll(t16, 8, 0), 0.0)
+            X[h, z * D + T:(z + 1) * D, part] = x16.astype(BF16)
+
+        def solve(z):
+            got = dot(P[z * D:(z + 1) * D, :], X[h])
+            for p in (0, 1):
+                idx = base + 2 * p + z
+                part = slice(p * LANES, (p + 1) * LANES)
+                end = 2 * p + z == (0 if low else L - 1)
+                t16 = R[h, idx, T:, :]
+                for q in range(5):
+                    if q < 4:
+                        at = class_rows(q)
+                        s = t16[8 + q:9 + q]
+                        k = t16[4 + q:5 + q]
+                    else:
+                        at = slice(T, D)
+                        s = jnp.where(row16 < 4, pltpu.roll(t16, 8, 0), 0.0)
+                        k = jnp.where(row16 < 4, pltpu.roll(t16, 12, 0), 0.0)
+                    c = got[at, part] * s
+                    if not (even and end):
+                        S[h, idx, at, :] += c
+                    cb = c.astype(BF16)
+                    B[h, z, at, part] = (c * k).astype(BF16)
+                    B[h, z, D + at.start:D + at.stop, part] = cb
+                    B[h, 1 - z, 4 * D + at.start:4 * D + at.stop, part] = cb
+
+        def neighbours(z):
+            c = B[h, z, D:2 * D, :]
+            t = c[T:]
+            r16 = lax.broadcasted_iota(jnp.int32, (16, 2 * LANES), 0)
+            xp = dot(jnp.concatenate([c[:2 * A], t], 0), XP[...])
+            xm = dot(jnp.concatenate([c[2 * A:T], t], 0), XM[...])
+            yp = dot(jnp.concatenate([c[:A], c[2 * A:3 * A], t], 0), YP[...])
+            ym = dot(jnp.concatenate([c[A:2 * A], c[3 * A:T], t], 0), YM[...])
+            o = 2 * D
+            B[h, z, o:o + 2 * A, :] = xp[:2 * A].astype(BF16)
+            B[h, z, o + 2 * A:o + T, :] = xm[:2 * A].astype(BF16)
+            B[h, z, o + T:o + D, :] = jnp.where(r16 < 2, xp[2 * A:], xm[2 * A:]).astype(BF16)
+            o = 3 * D
+            B[h, z, o:o + A, :] = yp[:A].astype(BF16)
+            B[h, z, o + A:o + 2 * A, :] = ym[:A].astype(BF16)
+            B[h, z, o + 2 * A:o + 3 * A, :] = yp[A:2 * A].astype(BF16)
+            B[h, z, o + 3 * A:o + T, :] = ym[A:2 * A].astype(BF16)
+            B[h, z, o + T:o + D, :] = jnp.where(r16 % 2 == 0, yp[2 * A:], ym[2 * A:]).astype(BF16)
+
+        def apply(z):
+            acc = dot(W[z], B[h, z])
+            for p in (0, 1):
+                R[h, base + 2 * p + z] += acc[:, p * LANES:(p + 1) * LANES]
+
+        solve(first)
+        c_copy(h, base, t, low).start()
+        solve(1 - first)
+        if last is not None:
+            @pl.when(last)
+            def _():
+                c2_copy(h, not low).start()
+        neighbours(first)
+        apply(first)
+        end = base if low else base + L - 1
+
+        def send_r():
+            rsb[h] = R[h, end].astype(BF16)
+            r_copy(h, base, t, low).start()
+
+        if last is None:
+            send_r()
+        else:
+            pl.when(jnp.logical_not(last))(send_r)
+        neighbours(1 - first)
+        apply(1 - first)
+        if low:
+            acc = z_down(B[h, 1, D:2 * D, :])
+            R[h, base + 2] += acc[:, :LANES]
+            new, out = acc[:, LANES:], base + L
+            R[h, base + 1] += z_up(B[h, 0, D:2 * D, LANES:])
+        else:
+            acc = z_up(B[h, 0, D:2 * D, :])
+            R[h, base + 1] += acc[:, LANES:]
+            new, out = acc[:, :LANES], base - 1
+            R[h, base + 2] += z_down(B[h, 1, D:2 * D, :LANES])
+        R[h, out, :T, :] = new[:T]
+        R[h, out, T:T + 4, :] = new[T:T + 4]
+
+    def finish(h, base, t, even, last):
+        low = base == 0
+        near, out = (base + L - 1, base + L) if low else (base, base - 1)
+        c_copy(h, base, t, low).wait()
+        c = cr[t, h]
+        R[h, near] += z_up(c) if low else z_down(c)
+        if even:
+            S[h, out] += c.astype(F32)
+
+        def take():
+            r_copy(h, base, t, low).wait()
+            R[h, out, :T, :] += rr[t, h, :T, :].astype(F32)
+            R[h, out, T:T + 4, :] += rr[t, h, T:, :].astype(F32)[:4]
+
+        if last is None:
+            take()
+        else:
+            pl.when(jnp.logical_not(last))(take)
+
+            @pl.when(last)
+            def _():
+                c2_copy(h, not low).wait()
+                other = base if low else base + L - 1
+                R[h, other] += z_down(cr2[h]) if low else z_up(cr2[h])
+
+    def between(h, u):
+        def shift(d, down):
+            for idx in range(L + 1):
+                move(R, h, idx, d, down)
+            for z in range(L):
+                move(S, h, z + 1 - h, d, down)
+
+        @pl.when(lax.rem(u, 2) == 0)
+        def _():
+            shift(1, False)
+
+        @pl.when(u == 1)
+        def _():
+            shift(0, False)
+            shift(1, True)
+
+    def body(u, carry):
+        begin(0, 0, 2 * u, True, None)
+
+        @pl.when(u > 0)
+        def _():
+            finish(1, 0, 2 * u - 1, False, None)
+            between(1, u - 1)
+
+        begin(1, 1, 2 * u, True, None)
+        finish(0, 0, 2 * u, True, None)
+        begin(0, 1, 2 * u + 1, False, u == 3)
+        finish(1, 1, 2 * u, True, None)
+        begin(1, 0, 2 * u + 1, False, u == 3)
+        finish(0, 1, 2 * u + 1, False, u == 3)
+
+        @pl.when(u < 3)
+        def _():
+            between(0, u)
+        return carry
+
+    lax.fori_loop(0, 4, body, 0)
+
+    def cut(ref, out):
+        for r in range(0, D, 16):
+            v = swap_source([ref[n % 2, n // 2 + 1 - n % 2, r:r + 16, :] for n in range(G)])
+            for n in range(G):
+                out[n, r:r + 16, :] = v[n].astype(BF16)
+
+    def ship(out, got, k):
+        sent = []
+        for o in range(1, G):
+            s, where = in_plane(o)
+            sent.append(remote(out.at[where["gx"] * ny + where["gy"]], got.at[slab], k + o, where))
+            sent[-1].start()
+        got[slab] = out[mine]
+        return sent
+
+    def unpack(got, out):
+        for q in range(4):
+            for r in range(0, A, 16):
+                v = swap_slab([got[s, q * A + r:q * A + r + 16, :].astype(F32) for s in range(G)])
+                for (i, j), x in zip(cells, v):
+                    out[2 * i + q // 2, 2 * j + q % 2, r:r + 16, :] = x
+        v = swap_slab([got[s, T:, :].astype(F32) for s in range(G)])
+        for (i, j), x in zip(cells, v):
+            for q in range(4):
+                out[2 * i + q // 2, 2 * j + q % 2, A:A + 1, :] = x[q:q + 1]
+
+    cut(S, osol)
+    first = ship(osol, rsol, 48)
+    finish(1, 0, 7, False, jnp.bool_(True))
+    cut(R, ores)
+    second = ship(ores, rres, 56)
+    for copy in first:
+        copy.wait()
+    unpack(rsol, sol_ref)
+    for copy in second:
+        copy.wait()
+    unpack(rres, res_ref)
+
+
+def in_slabs(sizes, right_side, cell_coef, cell_matrix, face_coupling, patch_inverse):
+    Q = cell_matrix.shape[0]
+    X, Y, Z = cell_coef.shape
+    lanes = right_side.shape[3]
+    nx, ny, nz = sizes
+    G = nx * ny
+    D = 4 * (Q - 1) + 16
+    start = jnp.transpose(right_side, (1, 2, 0, 3))
+    coef = jnp.repeat(cell_coef, lanes // Z, axis=2)
+    V = pltpu.VMEM
+    half = (D, LANES)
+    side = (2 * LANES, 2 * LANES)
+    scratch = [
+        V((G, *half), BF16), V((G, *half), BF16),
+        V((2, 5, *half), F32), V((2, 5, *half), F32),
+        V((2, 2 * D, 2 * LANES), BF16), V((2, 2, 5 * D, 2 * LANES), BF16),
+        V((2, D, 5 * D), BF16), V((2 * D, 2 * D), BF16),
+        V(side, BF16), V(side, BF16), V(side, BF16), V(side, BF16),
+        V((4 * 96, 4 * LANES), BF16), V((2 * D, 8 * Q), BF16),
+        V((8, 2, *half), BF16), V((8, 2, *half), BF16), V((2, *half), BF16), V((2, *half), BF16),
+        V((G, *half), BF16), V((G, *half), BF16), V((G, *half), BF16), V((G, *half), BF16),
+        pltpu.SemaphoreType.DMA((64,)), pltpu.SemaphoreType.DMA((64,)),
+    ]
+    vmem = pl.BlockSpec(memory_space=pltpu.VMEM)
+    sol, res = pl.pallas_call(
+        functools.partial(slab_kernel, sizes, (Q, nx, ny, nz, X // 2, Y // 2)),
+        out_shape=[jax.ShapeDtypeStruct((X, Y, Q, lanes), F32)] * 2,
+        in_specs=[vmem] * 5,
+        out_specs=[vmem] * 2,
+        scratch_shapes=scratch,
+        compiler_params=pltpu.CompilerParams(
+            collective_id=0, has_side_effects=True, vmem_limit_bytes=60 * 1024 * 1024),
+    )(start, coef, patch_inverse, cell_matrix, face_coupling)
+    return tuple(jnp.transpose(x, (2, 0, 1, 3)) for x in (sol, res))
+
+
+def on_device(sizes, right_side, cell_coef, cell_matrix, face_coupling, patch_inverse):
+    X, Y, Z = cell_coef.shape
+    form = in_slabs if fits_slabs(sizes, cell_matrix.shape[0], X, Y, Z, right_side.shape[3]) else in_blocks
+    return form(sizes, right_side, cell_coef, cell_matrix, face_coupling, patch_inverse)
 
 
 def solution(mesh):

time: 155 us -> 108 us (0.70)
  Pallas kernels: 143 us -> 97.8 us
  other arithmetic: 2.16 us -> 0 us
    pallas_call x1, Pallas kernels: 143 us -> 97.8 us  [in_slabs(): pl.pallas_call(functools.partial(slab_kernel, sizes, (Q, nx, ny, nz, X //...]
    unnamed x14 -> x6, local copies, waits for them, and re-layouts: 4.51 us -> 8.11 us
    transpose x1 -> x0, local copies, waits for them, and re-layouts: 2.02 us -> none  [on_device(): return tuple((jnp.transpose(x[:, :, :Q], (2, 0, 1, 3)) for x in (sol, res)))]
where the time goes in v1:
time: 108 us; the launch traced here: 107 us
  Pallas kernels  97.8 us (91%)
  local copies, waits for them, and re-layouts  8.86 us (8%)
    pallas_call x1, Pallas kernels, in_slabs(): pl.pallas_call(functools.partial(slab_kernel, sizes, (Q, nx, ny, nz, X //...  97.8 us
    unnamed x6, local copies, waits for them, and re-layouts  8.11 us

profile of v1, /device:TPU:0, one launch (start us, length us, event | category | flops | bytes accessed | tf_op | source)
XLA Modules:
  0.0 107.3 jit_solution(17371994133446324691)
XLA Ops:
  0.6 0.8 copy.11
  1.5 0.7 copy.12.coef_ref
  2.2 3.2 %copy.16 = f32[81,4,8,128]{3,0,2,1:T(8,128)} copy(f32[81,4,8,128]{3,2,1,0:T(8,128)} %param.5) | data formatting | bytes 2654208 | tf_op args[0]
  5.4 97.8 %shard_map.68 = (f32[4,8,81,128]{3,2,1,0:T(8,128)}, f32[4,8,81,128]{3,2,1,0:T(8,128)}) custom-call(f32[4,8,81,128]{3,2,1,0:T(8,128)} %bitcast.6, f32[4,8,128]{2,1,0:T(8,128)} %copy.12.coef_ref, bf16[648,648]{1,0:T(8,128)(2,1)} %inverse_ref.1, f32[81,81]{1,0:T(8,128)} %m_ref.1, f32[3,81,81]{2,1,0:T(8,128)} %f_ref.1), custom_call_target="tpu_custom_call" | custom-call | tf_op jit(solution)/shard_map/pallas_call | solution.py:918
  103.2 0.0 copy-start
  103.2 2.8 %copy.13 = f32[81,4,8,128]{3,2,1,0:T(8,128)} copy(f32[81,4,8,128]{3,0,2,1:T(8,128)} %bitcast.8) | data formatting | bytes 2654208
  106.0 0.0 copy-done
  106.0 1.3 %copy.14 = f32[81,4,8,128]{3,2,1,0:T(8,128)} copy(f32[81,4,8,128]{3,0,2,1:T(8,128)S(1)} %bitcast.7) | data formatting | bytes 2654208
  (1 shorter events, 0.0 us)
Async XLA Ops:
  103.2 2.8 %copy-start = (f32[4,8,81,128]{3,2,1,0:T(8,128)S(1)}, f32[4,8,81,128]{3,2,1,0:T(8,128)}, u32[]{:S(2)}) copy-start(f32[4,8,81,128]{3,2,1,0:T(8,128)} %get-tuple-element.5) | copy-start | bytes 3981316

commit v2 on v1

--- a/solution.py
+++ b/solution.py
@@ -411,9 +411,9 @@
             and X % 2 == 0 and Y % 2 == 0)
 
 
-def slab_kernel(sizes, dims, start_ref, coef_ref, inverse_ref, m_ref, f_ref, sol_ref, res_ref,
-                msg, rx, R, S, X, B, W, P, XP, XM, YP, YM, U, p_rows,
-                cr, rr, cr2, rsb, osol, ores, rsol, rres, send_sem, recv_sem):
+def slab_kernel(sizes, dims, right_ref, coef_ref, inverse_ref, m_ref, f_ref, sol_out, res_out,
+                start_ref, sol_ref, res_ref, coef_high, coef_low, msg, rx, R, S, X, B, W, P, XP, XM, YP, YM, U, p_rows,
+                cr, rr, cr2, rsb, osol, ores, rsol, rres, send_sem, recv_sem, load_sem, store_sem):
     Q, nx, ny, nz, hx, hy = dims
     G = nx * ny
     L = 4
@@ -450,6 +450,22 @@
         s = lax.rem(slab + o, G)
         return s, device(gz, s)
 
+    places = [(x, y) for x in range(2 * hx) for y in range(2 * hy)]
+
+    def local(src, dst, sem, k):
+        return pltpu.make_async_copy(src, dst, sem.at[k])
+
+    def load(k):
+        x, y = places[k]
+        return local(right_ref.at[:, x, y, :], start_ref.at[x, y], load_sem, k)
+
+    def store(ref, out, k, first):
+        x, y = places[k]
+        return local(ref.at[x, y], out.at[:, x, y, :], store_sem, first + k)
+
+    for k in range(len(places)):
+        load(k).start()
+
     barrier = pltpu.get_barrier_semaphore()
     for o in range(1, G):
         pl.semaphore_signal(barrier, inc=1, device_id=in_plane(o)[1], device_id_type=MESH)
@@ -522,33 +538,51 @@
         return slice(q * A, (q + 1) * A)
 
     cells = [(i, j) for i in range(hx) for j in range(hy)]
-
-    def tail_tile(i, j):
+    M = 2 * A + 16
+
+    def tail_tile(px, i, j):
         out = jnp.zeros((16, LANES), F32)
-        for q in range(4):
-            x, y = 2 * i + q // 2, 2 * j + q % 2
-            k = coef_ref[x, y:y + 1, :]
-            high = k.astype(BF16).astype(F32)
-            out = jnp.where(row16 == q, start_ref[x, y, A:A + 1, :], out)
-            out = jnp.where(row16 == 4 + q, high, out)
-            out = jnp.where(row16 == 8 + q, k - high, out)
+        for py in (0, 1):
+            x, y = 2 * i + px, 2 * j + py
+            at = slice(2 * hy * x + y, 2 * hy * x + y + 1)
+            out = jnp.where(row16 == py, start_ref[x, y, A:A + 1, :], out)
+            out = jnp.where(row16 == 4 + py, coef_high[at, :], out)
+            out = jnp.where(row16 == 8 + py, coef_low[at, :], out)
         return out
 
-    for q in range(4):
+    zs = coef_ref.shape[1]
+    spread = (lax.broadcasted_iota(jnp.int32, (zs, LANES), 1) // (LANES // zs)
+              == lax.broadcasted_iota(jnp.int32, (zs, LANES), 0))
+    spread = jnp.where(spread, 1.0, 0.0).astype(BF16)
+    high = coef_ref[...].astype(BF16)
+    low = (coef_ref[...] - high.astype(F32)).astype(BF16)
+    coef_high[...] = jnp.dot(high, spread, preferred_element_type=F32)
+    coef_low[...] = jnp.dot(low, spread, preferred_element_type=F32)
+    for k in range(len(places)):
+        load(k).wait()
+
+    def pack(tiles, at):
+        v = [swap_slab(t) for t in tiles]
+        for s in range(G):
+            for half, x in enumerate(swap([v[0][s], v[1][s]], 1, 2)):
+                msg[half, s, at, :] = x.astype(BF16)
+
+    for py in (0, 1):
         for r in range(0, A, 16):
-            v = swap_slab([start_ref[2 * i + q // 2, 2 * j + q % 2, r:r + 16, :] for i, j in cells])
-            for s in range(G):
-                msg[s, q * A + r:q * A + r + 16, :] = v[s].astype(BF16)
-    v = swap_slab([tail_tile(i, j) for i, j in cells])
-    for s in range(G):
-        msg[s, T:, :] = v[s].astype(BF16)
+            pack([[start_ref[2 * i + px, 2 * j + py, r:r + 16, :] for i, j in cells] for px in (0, 1)],
+                 slice(py * A + r, py * A + r + 16))
+    pack([[tail_tile(px, i, j) for i, j in cells] for px in (0, 1)], slice(2 * A, M))
     pl.semaphore_wait(barrier, G + 1)
     arrivals = []
-    for o in range(1, G):
-        s, where = in_plane(o)
-        arrivals.append(remote(msg.at[s], rx.at[mine], 32 + o, where))
-        arrivals[-1].start()
-    rx[mine] = msg[slab]
+    for half in (0, 1):
+        arrivals.append([])
+        for o in range(1, G):
+            s, where = in_plane(o)
+            arrivals[half].append(
+                remote(msg.at[half, s], rx.at[half, mine], 32 + G * half + o, where))
+            arrivals[half][-1].start()
+    for half in (0, 1):
+        rx[half, mine] = msg[half, slab]
 
     def dot(a, b):
         return jnp.dot(a, b, preferred_element_type=F32)
@@ -559,90 +593,93 @@
     def iota(shape, d):
         return lax.broadcasted_iota(jnp.int32, shape, d)
 
-    src, dst = iota((2 * LANES, 2 * LANES), 0), iota((2 * LANES, 2 * LANES), 1)
-    same = (src // LANES == dst // LANES) & (src % 2 == dst % 2)
-    sl, dl = src % LANES, dst % LANES
-    for ref, step in ((XP, 1), (XM, hx * nx - 1)):
-        hit = same & (lane_y(sl) == lane_y(dl)) & (lane_x(sl) == (lane_x(dl) + step) % (hx * nx))
-        ref[...] = jnp.where(hit, 1.0, 0.0).astype(BF16)
-    for ref, step in ((YP, 1), (YM, hy * ny - 1)):
-        hit = same & (lane_x(sl) == lane_x(dl)) & (lane_y(sl) == (lane_y(dl) + step) % (hy * ny))
-        ref[...] = jnp.where(hit, 1.0, 0.0).astype(BF16)
+    def one_hot(hit):
+        return jnp.where(hit, 1.0, 0.0).astype(BF16)
+
+    wide2 = 2 * LANES
+    src, dst = iota((wide2, 1), 0), iota((1, wide2), 1)
+
+    def column(l, x_step, y_step):
+        n = l % LANES
+        x, y = (lane_x(n) + x_step) % (hx * nx), (lane_y(n) + y_step) % (hy * ny)
+        return ((l // LANES * 2 + l % 2) * (hx * nx) + x) * (hy * ny) + y
+
+    for ref, x_step, y_step in ((XP, 1, 0), (XM, hx * nx - 1, 0), (YP, 0, 1), (YM, 0, hy * ny - 1)):
+        ref[...] = one_hot(column(src, 0, 0) == column(dst, x_step, y_step))
 
     def patch_row(k):
         d, c = k // 8, k % 8
         return c % 2 * D + jnp.where(d < A, c // 2 * A + d, T + c // 2)
 
-    pick = patch_row(iota((2 * D, 8 * Q), 1)) == iota((2 * D, 8 * Q), 0)
-    p_rows[...] = dot(jnp.where(pick, 1.0, 0.0).astype(BF16), inverse_ref[...]).astype(BF16)
-    pick = patch_row(iota((8 * Q, 2 * D), 0)) == iota((8 * Q, 2 * D), 1)
-    P[...] = dot(p_rows[...], jnp.where(pick, 1.0, 0.0).astype(BF16)).astype(BF16)
-
-    def packed(k, n):
-        q, d = k // n, k % n
+    pick = one_hot(patch_row(iota((1, 8 * Q), 1)) == iota((2 * D, 8 * Q), 0))
+    p_rows[...] = dot(pick, inverse_ref[...]).astype(BF16)
+    pick = one_hot(patch_row(iota((8 * Q, 1), 0)) == iota((8 * Q, 2 * D), 1))
+    P[...] = dot(p_rows[...], pick).astype(BF16)
+
+    def packed(k):
+        q, d = k // LANES, k % LANES
         return jnp.where(d < A, q * A + d, jnp.where(d == A, T + q, -1))
 
-    def one_hot(hit):
-        return jnp.where(hit, 1.0, 0.0).astype(BF16)
-
-    NR, NC = U.shape[0] // 4, U.shape[1] // 4
-    rows_r = one_hot(packed(iota((D, 4 * NR), 1), NR) == iota((D, 4 * NR), 0))
-    rows_c = one_hot(packed(iota((D, 4 * NC), 1), NC) == iota((D, 4 * NC), 0))
-    cols_r = one_hot(packed(iota((4 * NR, D), 0), NR) == iota((4 * NR, D), 1))
-    cols_c = one_hot(packed(iota((4 * NC, D), 0), NC) == iota((4 * NC, D), 1))
+    cols = one_hot(packed(iota((4 * LANES, 1), 0)) == iota((4 * LANES, D), 1))
+    eye = one_hot(iota((D, 1), 0) == iota((D, D), 1))
 
     def table(blocks):
         U[...] = jnp.zeros_like(U)
         for a, b, m in blocks:
-            U[a * NR:a * NR + Q, b * NC:b * NC + Q] = m.astype(BF16)
-
-    def plain():
-        return dot(dot(rows_r, U[...]).astype(BF16), cols_c)
-
-    def turned():
-        return dot(dot_t(rows_c, U[...]).astype(BF16), cols_r)
+            U[a * A:(a + 1) * A, b * LANES:b * LANES + Q] = m[:A]
+            U[T + a:T + a + 1, b * LANES:b * LANES + Q] = m[A:]
+        return dot(U[...].astype(BF16), cols).astype(BF16)
+
+    def turned(w):
+        return dot_t(eye, w).astype(BF16)
 
     fx, fy, fz = f_ref[0], f_ref[1], f_ref[2]
-    table([(q, q, -m_ref[...]) for q in range(4)])
-    w = plain().astype(BF16)
-    W[0, :, :D] = w
-    W[1, :, :D] = w
-    table([(0, 2, fx), (1, 3, fx), (0, 1, fy), (2, 3, fy)])
-    w = (plain() + turned()).astype(BF16)
-    W[0, :, D:2 * D] = w
-    W[1, :, D:2 * D] = w
-    table([(2, 0, fx), (3, 1, fx)])
-    w = (plain() + turned()).astype(BF16)
-    W[0, :, 2 * D:3 * D] = w
-    W[1, :, 2 * D:3 * D] = w
-    table([(1, 0, fy), (3, 2, fy)])
-    w = (plain() + turned()).astype(BF16)
-    W[0, :, 3 * D:4 * D] = w
-    W[1, :, 3 * D:4 * D] = w
-    table([(q, q, fz) for q in range(4)])
-    W[0, :, 4 * D:] = plain().astype(BF16)
-    W[1, :, 4 * D:] = turned().astype(BF16)
+    order = ((0, 1, 2, 3, 4), (2, 3, 4, 1, 0))
+
+    def put(k, w):
+        for z in (0, 1):
+            W[z, :, order[z][k] * D:(order[z][k] + 1) * D] = w[z]
+
+    w = table([(q, q, -m_ref[...]) for q in range(4)])
+    put(0, (w, w))
+    w = table([(2, 0, fx), (3, 1, fx)])
+    w += turned(w)
+    put(1, (w, w))
+    w = table([(1, 0, fy), (3, 2, fy)])
+    w += turned(w)
+    put(2, (w, w))
+    w = table([(0, 2, fx), (1, 3, fx), (0, 1, fy), (2, 3, fy)])
+    w += turned(w)
+    put(3, (w, w))
+    w = table([(q, q, fz) for q in range(4)])
+    put(4, (w, turned(w)))
     S[...] = jnp.zeros_like(S)
 
     def z_up(c):
         return dot(W[0, :, 4 * D:], c)
 
     def z_down(c):
-        return dot(W[1, :, 4 * D:], c)
-
-    for copy in arrivals:
-        copy.wait()
-    for r in range(0, D, 16):
-        v = swap_source([rx[n, r:r + 16, :].astype(F32) for n in range(G)])
-        for n in range(G):
-            z, h = n // 2, n % 2
-            R[h, z + 1 - h, r:r + 16, :] = v[n]
-
-    def move(ref, h, idx, d, down):
+        return dot(W[1, :, :D], c)
+
+    def arrive(h):
+        for copy in arrivals[h]:
+            copy.wait()
+        for py in (0, 1):
+            for r in range(0, A, 16):
+                at = slice(py * A + r, py * A + r + 16)
+                v = swap_source([rx[h, n, at, :].astype(F32) for n in range(G)])
+                for n in range(G):
+                    first = (n % 2 * 2 + py) * A + r
+                    R[h, n // 2 + 1 - h, first:first + 16, :] = v[n]
+        v = swap_source([rx[h, n, 2 * A:, :].astype(F32) for n in range(G)])
+        for z in range(L):
+            R[h, z + 1 - h, T:, :] = jnp.where(row16 % 4 < 2, v[2 * z], pltpu.roll(v[2 * z + 1], 2, 0))
+
+    def move(ref, h, idx, d, down, only_tail=False):
         shift = shift_x if d == 0 else shift_y
         bit = 2 >> d
         for q in range(4):
-            if q & bit:
+            if q & bit or only_tail:
                 continue
             old0 = ref[h, idx, class_rows(q), :]
             old1 = ref[h, idx, class_rows(q + bit), :]
@@ -660,18 +697,22 @@
             t = jnp.where(upper, t, shift(t, 1))
         ref[h, idx, T:, :] = jnp.where(upper, pltpu.roll(t, bit, 0), pltpu.roll(t, 16 - bit, 0))
 
-    copies = []
-    for h in (0, 1):
-        for z in range(L):
+    def first_copy(h):
+        return remote(rsb.at[h], rr.at[7, h], 60 + h, ring(1 if h == 0 else -1))
+
+    def enter(h):
+        arrive(h)
+        end = L if h == 0 else 0
+        for idx in [end] + [z + 1 - h for z in range(L) if z + 1 - h != end]:
             for d in (0, 1):
-                move(R, h, z + 1 - h, d, True)
-        end, step = (L, 1) if h == 0 else (0, -1)
-        rsb[h] = R[h, end].astype(BF16)
-        copies.append(remote(rsb.at[h], cr2.at[h], 40 + h, ring(step)))
-        copies[-1].start()
-    for h in (0, 1):
-        copies[h].wait()
-        R[h, 0 if h == 0 else L] = cr2[h].astype(F32)
+                move(R, h, idx, d, True)
+            if idx == end:
+                rsb[h] = R[h, end].astype(BF16)
+                first_copy(h).start()
+
+    def settle(h):
+        first_copy(h).wait()
+        R[h, 0 if h == 0 else L] = rr[7, h].astype(F32)
         for idx in range(L + 1):
             t = R[h, idx, T:, :]
             k = t + pltpu.roll(t, 12, 0)
@@ -680,19 +721,27 @@
             t = jnp.where(row16 < 4, t, jnp.where(row16 < 8, k, jnp.where(row16 < 12, s, 0.0)))
             R[h, idx, T:, :] = t
 
+    enter(0)
+    enter(1)
+    settle(0)
+
     def split(k):
         return k % 2, slice(k // 2 * LANES, (k // 2 + 1) * LANES)
 
+    def block(z, k):
+        n = 3 * z + order[z][k]
+        return slice(n * D, (n + 1) * D)
+
     def c_copy(h, base, t, low):
         z, part = split(0 if low else L - 1)
-        return remote(B.at[h, z, D:2 * D, part], cr.at[t, h], t * 4 + h, ring(-1 if low else 1))
+        return remote(B.at[h, block(z, 3), part], cr.at[t, h], t * 4 + h, ring(-1 if low else 1))
 
     def r_copy(h, base, t, low):
         return remote(rsb.at[h], rr.at[t, h], t * 4 + 2 + h, ring(-1 if low else 1))
 
     def c2_copy(h, low):
         z, part = split(0 if low else L - 1)
-        return remote(B.at[h, z, D:2 * D, part], cr2.at[h], 42 + h, ring(-1 if low else 1))
+        return remote(B.at[h, block(z, 3), part], cr2.at[h], 62 + h, ring(-1 if low else 1))
 
     def begin(h, base, t, even, last):
         low = base == 0
@@ -727,31 +776,31 @@
                     if not (even and end):
                         S[h, idx, at, :] += c
                     cb = c.astype(BF16)
-                    B[h, z, at, part] = (c * k).astype(BF16)
-                    B[h, z, D + at.start:D + at.stop, part] = cb
-                    B[h, 1 - z, 4 * D + at.start:4 * D + at.stop, part] = cb
+                    own, cor = block(z, 0).start, block(z, 3).start
+                    B[h, own + at.start:own + at.stop, part] = (c * k).astype(BF16)
+                    B[h, cor + at.start:cor + at.stop, part] = cb
 
         def neighbours(z):
-            c = B[h, z, D:2 * D, :]
+            c = B[h, block(z, 3), :]
             t = c[T:]
             r16 = lax.broadcasted_iota(jnp.int32, (16, 2 * LANES), 0)
             xp = dot(jnp.concatenate([c[:2 * A], t], 0), XP[...])
             xm = dot(jnp.concatenate([c[2 * A:T], t], 0), XM[...])
             yp = dot(jnp.concatenate([c[:A], c[2 * A:3 * A], t], 0), YP[...])
             ym = dot(jnp.concatenate([c[A:2 * A], c[3 * A:T], t], 0), YM[...])
-            o = 2 * D
-            B[h, z, o:o + 2 * A, :] = xp[:2 * A].astype(BF16)
-            B[h, z, o + 2 * A:o + T, :] = xm[:2 * A].astype(BF16)
-            B[h, z, o + T:o + D, :] = jnp.where(r16 < 2, xp[2 * A:], xm[2 * A:]).astype(BF16)
-            o = 3 * D
-            B[h, z, o:o + A, :] = yp[:A].astype(BF16)
-            B[h, z, o + A:o + 2 * A, :] = ym[:A].astype(BF16)
-            B[h, z, o + 2 * A:o + 3 * A, :] = yp[A:2 * A].astype(BF16)
-            B[h, z, o + 3 * A:o + T, :] = ym[A:2 * A].astype(BF16)
-            B[h, z, o + T:o + D, :] = jnp.where(r16 % 2 == 0, yp[2 * A:], ym[2 * A:]).astype(BF16)
+            o = block(z, 1).start
+            B[h, o:o + 2 * A, :] = xp[:2 * A].astype(BF16)
+            B[h, o + 2 * A:o + T, :] = xm[:2 * A].astype(BF16)
+            B[h, o + T:o + D, :] = jnp.where(r16 < 2, xp[2 * A:], xm[2 * A:]).astype(BF16)
+            o = block(z, 2).start
+            B[h, o:o + A, :] = yp[:A].astype(BF16)
+            B[h, o + A:o + 2 * A, :] = ym[:A].astype(BF16)
+            B[h, o + 2 * A:o + 3 * A, :] = yp[A:2 * A].astype(BF16)
+            B[h, o + 3 * A:o + T, :] = ym[A:2 * A].astype(BF16)
+            B[h, o + T:o + D, :] = jnp.where(r16 % 2 == 0, yp[2 * A:], ym[2 * A:]).astype(BF16)
 
         def apply(z):
-            acc = dot(W[z], B[h, z])
+            acc = dot(W[z], B[h, 3 * z * D:(3 * z + 5) * D, :])
             for p in (0, 1):
                 R[h, base + 2 * p + z] += acc[:, p * LANES:(p + 1) * LANES]
 
@@ -777,15 +826,15 @@
         neighbours(1 - first)
         apply(1 - first)
         if low:
-            acc = z_down(B[h, 1, D:2 * D, :])
+            acc = z_down(B[h, block(1, 3), :])
             R[h, base + 2] += acc[:, :LANES]
             new, out = acc[:, LANES:], base + L
-            R[h, base + 1] += z_up(B[h, 0, D:2 * D, LANES:])
+            R[h, base + 1] += z_up(B[h, block(0, 3), LANES:])
         else:
-            acc = z_up(B[h, 0, D:2 * D, :])
+            acc = z_up(B[h, block(0, 3), :])
             R[h, base + 1] += acc[:, LANES:]
             new, out = acc[:, :LANES], base - 1
-            R[h, base + 2] += z_down(B[h, 1, D:2 * D, :LANES])
+            R[h, base + 2] += z_down(B[h, block(1, 3), :LANES])
         R[h, out, :T, :] = new[:T]
         R[h, out, T:T + 4, :] = new[T:T + 4]
 
@@ -817,7 +866,7 @@
     def between(h, u):
         def shift(d, down):
             for idx in range(L + 1):
-                move(R, h, idx, d, down)
+                move(R, h, idx, d, down, idx == (L if h == 0 else 0))
             for z in range(L):
                 move(S, h, z + 1 - h, d, down)
 
@@ -830,6 +879,30 @@
             shift(0, False)
             shift(1, True)
 
+    def out_copy(out, got, h, kind, o):
+        s, where = in_plane(o)
+        return remote(out.at[h, where["gx"] * ny + where["gy"]], got.at[h, slab],
+                      64 + (2 * kind + h) * G + o, where)
+
+    def send_out(ref, h, out, got, kind):
+        for py in (0, 1):
+            for r in range(0, A, 16):
+                v = []
+                for n in range(G):
+                    first = (n % 2 * 2 + py) * A + r
+                    v.append(ref[h, n // 2 + 1 - h, first:first + 16, :])
+                for n, x in enumerate(swap_source(v)):
+                    out[h, n, py * A + r:py * A + r + 16, :] = x.astype(BF16)
+        v = []
+        for n in range(G):
+            t = ref[h, n // 2 + 1 - h, T:, :]
+            v.append(pltpu.roll(t, 14, 0) if n % 2 else t)
+        for n, x in enumerate(swap_source(v)):
+            out[h, n, 2 * A:, :] = x.astype(BF16)
+        for o in range(1, G):
+            out_copy(out, got, h, kind, o).start()
+        got[h, slab] = out[h, mine]
+
     def body(u, carry):
         begin(0, 0, 2 * u, True, None)
 
@@ -838,12 +911,16 @@
             finish(1, 0, 2 * u - 1, False, None)
             between(1, u - 1)
 
+        pl.when(u == 0)(lambda: settle(1))
         begin(1, 1, 2 * u, True, None)
         finish(0, 0, 2 * u, True, None)
         begin(0, 1, 2 * u + 1, False, u == 3)
+        pl.when(u == 3)(lambda: send_out(S, 0, osol, rsol, 0))
         finish(1, 1, 2 * u, True, None)
         begin(1, 0, 2 * u + 1, False, u == 3)
+        pl.when(u == 3)(lambda: send_out(S, 1, osol, rsol, 0))
         finish(0, 1, 2 * u + 1, False, u == 3)
+        pl.when(u == 3)(lambda: send_out(R, 0, ores, rres, 1))
 
         @pl.when(u < 3)
         def _():
@@ -852,43 +929,43 @@
 
     lax.fori_loop(0, 4, body, 0)
 
-    def cut(ref, out):
-        for r in range(0, D, 16):
-            v = swap_source([ref[n % 2, n // 2 + 1 - n % 2, r:r + 16, :] for n in range(G)])
-            for n in range(G):
-                out[n, r:r + 16, :] = v[n].astype(BF16)
-
-    def ship(out, got, k):
-        sent = []
+    finish(1, 0, 7, False, jnp.bool_(True))
+    send_out(R, 1, ores, rres, 1)
+
+    def unpack(got, out):
+        def merge(at):
+            pairs = [swap([got[0, s, at, :].astype(F32), got[1, s, at, :].astype(F32)], 1, 2)
+                     for s in range(G)]
+            return [swap_slab([p[px] for p in pairs]) for px in (0, 1)]
+
+        for py in (0, 1):
+            for r in range(0, A, 16):
+                v = merge(slice(py * A + r, py * A + r + 16))
+                for px in (0, 1):
+                    for (i, j), x in zip(cells, v[px]):
+                        out[2 * i + px, 2 * j + py, r:r + 16, :] = x
+        v = merge(slice(2 * A, M))
+        for px in (0, 1):
+            for (i, j), x in zip(cells, v[px]):
+                for py in (0, 1):
+                    out[2 * i + px, 2 * j + py, A:A + 1, :] = x[py:py + 1]
+
+    n = len(places)
+    for h in (0, 1):
         for o in range(1, G):
-            s, where = in_plane(o)
-            sent.append(remote(out.at[where["gx"] * ny + where["gy"]], got.at[slab], k + o, where))
-            sent[-1].start()
-        got[slab] = out[mine]
-        return sent
-
-    def unpack(got, out):
-        for q in range(4):
-            for r in range(0, A, 16):
-                v = swap_slab([got[s, q * A + r:q * A + r + 16, :].astype(F32) for s in range(G)])
-                for (i, j), x in zip(cells, v):
-                    out[2 * i + q // 2, 2 * j + q % 2, r:r + 16, :] = x
-        v = swap_slab([got[s, T:, :].astype(F32) for s in range(G)])
-        for (i, j), x in zip(cells, v):
-            for q in range(4):
-                out[2 * i + q // 2, 2 * j + q % 2, A:A + 1, :] = x[q:q + 1]
-
-    cut(S, osol)
-    first = ship(osol, rsol, 48)
-    finish(1, 0, 7, False, jnp.bool_(True))
-    cut(R, ores)
-    second = ship(ores, rres, 56)
-    for copy in first:
-        copy.wait()
+            out_copy(osol, rsol, h, 0, o).wait()
     unpack(rsol, sol_ref)
-    for copy in second:
-        copy.wait()
+    for k in range(n):
+        store(sol_ref, sol_out, k, 0).start()
+    for h in (0, 1):
+        for o in range(1, G):
+            out_copy(ores, rres, h, 1, o).wait()
     unpack(rres, res_ref)
+    for k in range(n):
+        store(res_ref, res_out, k, n).start()
+    for k in range(n):
+        store(sol_ref, sol_out, k, 0).wait()
+        store(res_ref, res_out, k, n).wait()
 
 
 def in_slabs(sizes, right_side, cell_coef, cell_matrix, face_coupling, patch_inverse):
@@ -898,33 +975,36 @@
     nx, ny, nz = sizes
     G = nx * ny
     D = 4 * (Q - 1) + 16
-    start = jnp.transpose(right_side, (1, 2, 0, 3))
-    coef = jnp.repeat(cell_coef, lanes // Z, axis=2)
+    coef = cell_coef.reshape(X * Y, Z)
     V = pltpu.VMEM
     half = (D, LANES)
     side = (2 * LANES, 2 * LANES)
+    block = (X, Y, Q, lanes)
+    piece = (2, G, 2 * (Q - 1) + 16, LANES)
     scratch = [
-        V((G, *half), BF16), V((G, *half), BF16),
+        V(block, F32), V(block, F32), V(block, F32), V((X * Y, lanes), F32), V((X * Y, lanes), F32),
+        V(piece, BF16), V(piece, BF16),
         V((2, 5, *half), F32), V((2, 5, *half), F32),
-        V((2, 2 * D, 2 * LANES), BF16), V((2, 2, 5 * D, 2 * LANES), BF16),
+        V((2, 2 * D, 2 * LANES), BF16), V((2, 8 * D, 2 * LANES), BF16),
         V((2, D, 5 * D), BF16), V((2 * D, 2 * D), BF16),
         V(side, BF16), V(side, BF16), V(side, BF16), V(side, BF16),
-        V((4 * 96, 4 * LANES), BF16), V((2 * D, 8 * Q), BF16),
+        V((D, 4 * LANES), F32), V((2 * D, 8 * Q), BF16),
         V((8, 2, *half), BF16), V((8, 2, *half), BF16), V((2, *half), BF16), V((2, *half), BF16),
-        V((G, *half), BF16), V((G, *half), BF16), V((G, *half), BF16), V((G, *half), BF16),
-        pltpu.SemaphoreType.DMA((64,)), pltpu.SemaphoreType.DMA((64,)),
+        V(piece, BF16), V(piece, BF16), V(piece, BF16), V(piece, BF16),
+        pltpu.SemaphoreType.DMA((96,)), pltpu.SemaphoreType.DMA((96,)),
+        pltpu.SemaphoreType.DMA((X * Y,)), pltpu.SemaphoreType.DMA((2 * X * Y,)),
     ]
     vmem = pl.BlockSpec(memory_space=pltpu.VMEM)
     sol, res = pl.pallas_call(
         functools.partial(slab_kernel, sizes, (Q, nx, ny, nz, X // 2, Y // 2)),
-        out_shape=[jax.ShapeDtypeStruct((X, Y, Q, lanes), F32)] * 2,
-        in_specs=[vmem] * 5,
-        out_specs=[vmem] * 2,
+        out_shape=[jax.ShapeDtypeStruct(right_side.shape, F32)] * 2,
+        in_specs=[pl.BlockSpec(memory_space=pl.ANY)] + [vmem] * 4,
+        out_specs=[pl.BlockSpec(memory_space=pl.ANY)] * 2,
         scratch_shapes=scratch,
         compiler_params=pltpu.CompilerParams(
             collective_id=0, has_side_effects=True, vmem_limit_bytes=60 * 1024 * 1024),
-    )(start, coef, patch_inverse, cell_matrix, face_coupling)
-    return tuple(jnp.transpose(x, (2, 0, 1, 3)) for x in (sol, res))
+    )(right_side, coef, patch_inverse, cell_matrix, face_coupling)
+    return sol, res
 
 
 def on_device(sizes, right_side, cell_coef, cell_matrix, face_coupling, patch_inverse):

time: 108 us -> 98.7 us (0.914)
  local copies, waits for them, and re-layouts: 8.86 us -> 3.65 us
  Pallas kernels: 97.8 us -> 94.1 us
    unnamed x6 -> x4, local copies, waits for them, and re-layouts: 8.11 us -> 3.65 us
    pallas_call x1, Pallas kernels: 97.8 us -> 94.1 us  [in_slabs(): pl.pallas_call(functools.partial(slab_kernel, sizes, (Q, nx, ny, nz, X //...]
where the time goes in v2:
time: 98.7 us; the launch traced here: 98.4 us
  Pallas kernels  94.1 us (95%)
  local copies, waits for them, and re-layouts  3.65 us (4%)
    pallas_call x1, Pallas kernels, in_slabs(): pl.pallas_call(functools.partial(slab_kernel, sizes, (Q, nx, ny, nz, X //...  94.1 us
    unnamed x4, local copies, waits for them, and re-layouts  3.65 us

profile of v2, /device:TPU:0, one launch (start us, length us, event | category | flops | bytes accessed | tf_op | source)
XLA Modules:
  0.0 98.4 jit_solution(3629079153871814855)
XLA Ops:
  0.6 94.1 %shard_map.68 = (f32[81,4,8,128]{3,2,1,0:T(8,128)}, f32[81,4,8,128]{3,2,1,0:T(8,128)}) custom-call(f32[81,4,8,128]{3,2,1,0:T(8,128)} %right_ref.1, f32[32,32]{1,0:T(8,128)} %bitcast.1, bf16[648,648]{1,0:T(8,128)(2,1)} %inverse_ref.1, f32[81,81]{1,0:T(8,128)} %m_ref.1, f32[3,81,81]{2,1,0:T(8,128)} %f_ref.1), custom_call_target="tpu_custom_call" | custom-call | tf_op jit(solution)/shard_map/pallas_call | solution.py:998
  94.8 0.0 copy-start
  94.8 2.6 %copy.9 = f32[81,4,8,128]{3,2,1,0:T(8,128)} copy(f32[81,4,8,128]{3,2,1,0:T(8,128)} %get-tuple-element.4) | data formatting | bytes 2654208
  97.3 0.0 copy-done
  97.3 1.1 %copy.10 = f32[81,4,8,128]{3,2,1,0:T(8,128)} copy(f32[81,4,8,128]{3,2,1,0:T(8,128)S(1)} %copy-done) | data formatting | bytes 2654208
Async XLA Ops:
  94.8 2.6 %copy-start = (f32[81,4,8,128]{3,2,1,0:T(8,128)S(1)}, f32[81,4,8,128]{3,2,1,0:T(8,128)}, u32[]{:S(2)}) copy-start(f32[81,4,8,128]{3,2,1,0:T(8,128)} %get-tuple-element.5) | copy-start | bytes 3981316

commit v3 on v2

--- a/solution.py
+++ b/solution.py
@@ -398,7 +398,7 @@
         out_specs=[vmem] * 2,
         scratch_shapes=scratch,
         compiler_params=pltpu.CompilerParams(
-            collective_id=0, has_side_effects=True, vmem_limit_bytes=60 * 1024 * 1024),
+            collective_id=0, has_side_effects=True, vmem_limit_bytes=46 * 1024 * 1024),
     )(start, patch_inverse, mats)
     return tuple(jnp.transpose(x[:, :, :Q], (2, 0, 1, 3)) for x in (sol, res))
 
@@ -411,9 +411,9 @@
             and X % 2 == 0 and Y % 2 == 0)
 
 
-def slab_kernel(sizes, dims, right_ref, coef_ref, inverse_ref, m_ref, f_ref, sol_out, res_out,
-                start_ref, sol_ref, res_ref, coef_high, coef_low, msg, rx, R, S, X, B, W, P, XP, XM, YP, YM, U, p_rows,
-                cr, rr, cr2, rsb, osol, ores, rsol, rres, send_sem, recv_sem, load_sem, store_sem):
+def slab_kernel(sizes, dims, start_ref, coef_ref, inverse_ref, m_ref, f_ref, sol_ref, res_ref,
+                coef_high, coef_low, msg, rx, R, S, X, B, W, P, XP, XM, YP, YM, U, p_rows,
+                cr, rr, cr2, rsb, osol, ores, rsol, rres, send_sem, recv_sem):
     Q, nx, ny, nz, hx, hy = dims
     G = nx * ny
     L = 4
@@ -450,22 +450,6 @@
         s = lax.rem(slab + o, G)
         return s, device(gz, s)
 
-    places = [(x, y) for x in range(2 * hx) for y in range(2 * hy)]
-
-    def local(src, dst, sem, k):
-        return pltpu.make_async_copy(src, dst, sem.at[k])
-
-    def load(k):
-        x, y = places[k]
-        return local(right_ref.at[:, x, y, :], start_ref.at[x, y], load_sem, k)
-
-    def store(ref, out, k, first):
-        x, y = places[k]
-        return local(ref.at[x, y], out.at[:, x, y, :], store_sem, first + k)
-
-    for k in range(len(places)):
-        load(k).start()
-
     barrier = pltpu.get_barrier_semaphore()
     for o in range(1, G):
         pl.semaphore_signal(barrier, inc=1, device_id=in_plane(o)[1], device_id_type=MESH)
@@ -558,8 +542,6 @@
     low = (coef_ref[...] - high.astype(F32)).astype(BF16)
     coef_high[...] = jnp.dot(high, spread, preferred_element_type=F32)
     coef_low[...] = jnp.dot(low, spread, preferred_element_type=F32)
-    for k in range(len(places)):
-        load(k).wait()
 
     def pack(tiles, at):
         v = [swap_slab(t) for t in tiles]
@@ -815,35 +797,37 @@
         apply(first)
         end = base if low else base + L - 1
 
-        def send_r():
-            rsb[h] = R[h, end].astype(BF16)
+        rsb[h] = R[h, end].astype(BF16)
+        if last is None:
             r_copy(h, base, t, low).start()
-
-        if last is None:
-            send_r()
         else:
-            pl.when(jnp.logical_not(last))(send_r)
+            pl.when(jnp.logical_not(last))(lambda: r_copy(h, base, t, low).start())
         neighbours(1 - first)
         apply(1 - first)
         if low:
             acc = z_down(B[h, block(1, 3), :])
             R[h, base + 2] += acc[:, :LANES]
             new, out = acc[:, LANES:], base + L
-            R[h, base + 1] += z_up(B[h, block(0, 3), LANES:])
         else:
             acc = z_up(B[h, block(0, 3), :])
             R[h, base + 1] += acc[:, LANES:]
             new, out = acc[:, :LANES], base - 1
-            R[h, base + 2] += z_down(B[h, block(1, 3), :LANES])
         R[h, out, :T, :] = new[:T]
         R[h, out, T:T + 4, :] = new[T:T + 4]
 
     def finish(h, base, t, even, last):
         low = base == 0
-        near, out = (base + L - 1, base + L) if low else (base, base - 1)
+        out = base + L if low else base - 1
         c_copy(h, base, t, low).wait()
         c = cr[t, h]
-        R[h, near] += z_up(c) if low else z_down(c)
+        if low:
+            acc = z_up(jnp.concatenate([B[h, block(0, 3), LANES:], c], 1))
+            R[h, base + 1] += acc[:, :LANES]
+            R[h, base + L - 1] += acc[:, LANES:]
+        else:
+            acc = z_down(jnp.concatenate([c, B[h, block(1, 3), :LANES]], 1))
+            R[h, base] += acc[:, :LANES]
+            R[h, base + 2] += acc[:, LANES:]
         if even:
             S[h, out] += c.astype(F32)
 
@@ -950,22 +934,14 @@
                 for py in (0, 1):
                     out[2 * i + px, 2 * j + py, A:A + 1, :] = x[py:py + 1]
 
-    n = len(places)
     for h in (0, 1):
         for o in range(1, G):
             out_copy(osol, rsol, h, 0, o).wait()
     unpack(rsol, sol_ref)
-    for k in range(n):
-        store(sol_ref, sol_out, k, 0).start()
     for h in (0, 1):
         for o in range(1, G):
             out_copy(ores, rres, h, 1, o).wait()
     unpack(rres, res_ref)
-    for k in range(n):
-        store(res_ref, res_out, k, n).start()
-    for k in range(n):
-        store(sol_ref, sol_out, k, 0).wait()
-        store(res_ref, res_out, k, n).wait()
 
 
 def in_slabs(sizes, right_side, cell_coef, cell_matrix, face_coupling, patch_inverse):
@@ -982,7 +958,7 @@
     block = (X, Y, Q, lanes)
     piece = (2, G, 2 * (Q - 1) + 16, LANES)
     scratch = [
-        V(block, F32), V(block, F32), V(block, F32), V((X * Y, lanes), F32), V((X * Y, lanes), F32),
+        V((X * Y, lanes), F32), V((X * Y, lanes), F32),
         V(piece, BF16), V(piece, BF16),
         V((2, 5, *half), F32), V((2, 5, *half), F32),
         V((2, 2 * D, 2 * LANES), BF16), V((2, 8 * D, 2 * LANES), BF16),
@@ -992,19 +968,18 @@
         V((8, 2, *half), BF16), V((8, 2, *half), BF16), V((2, *half), BF16), V((2, *half), BF16),
         V(piece, BF16), V(piece, BF16), V(piece, BF16), V(piece, BF16),
         pltpu.SemaphoreType.DMA((96,)), pltpu.SemaphoreType.DMA((96,)),
-        pltpu.SemaphoreType.DMA((X * Y,)), pltpu.SemaphoreType.DMA((2 * X * Y,)),
     ]
     vmem = pl.BlockSpec(memory_space=pltpu.VMEM)
     sol, res = pl.pallas_call(
         functools.partial(slab_kernel, sizes, (Q, nx, ny, nz, X // 2, Y // 2)),
-        out_shape=[jax.ShapeDtypeStruct(right_side.shape, F32)] * 2,
-        in_specs=[pl.BlockSpec(memory_space=pl.ANY)] + [vmem] * 4,
-        out_specs=[pl.BlockSpec(memory_space=pl.ANY)] * 2,
+        out_shape=[jax.ShapeDtypeStruct(block, F32)] * 2,
+        in_specs=[vmem] * 5,
+        out_specs=[vmem] * 2,
         scratch_shapes=scratch,
         compiler_params=pltpu.CompilerParams(
-            collective_id=0, has_side_effects=True, vmem_limit_bytes=60 * 1024 * 1024),
-    )(right_side, coef, patch_inverse, cell_matrix, face_coupling)
-    return sol, res
+            collective_id=0, has_side_effects=True, vmem_limit_bytes=46 * 1024 * 1024),
+    )(jnp.transpose(right_side, (1, 2, 0, 3)), coef, patch_inverse, cell_matrix, face_coupling)
+    return tuple(jnp.transpose(x, (2, 0, 1, 3)) for x in (sol, res))
 
 
 def on_device(sizes, right_side, cell_coef, cell_matrix, face_coupling, patch_inverse):

time: 98.7 us -> 94.5 us (0.957)
  Pallas kernels: 94.1 us -> 88.9 us
  local copies, waits for them, and re-layouts: 3.65 us -> 4.8 us
    pallas_call x1, Pallas kernels: 94.1 us -> 88.9 us  [in_slabs(): pl.pallas_call(functools.partial(slab_kernel, sizes, (Q, nx, ny, nz, X //...]
    unnamed x4 -> x11, local copies, waits for them, and re-layouts: 3.65 us -> 4.8 us
where the time goes in v3:
time: 94.5 us; the launch traced here: 94.4 us
  Pallas kernels  88.9 us (94%)
  local copies, waits for them, and re-layouts  4.8 us (5%)
    pallas_call x1, Pallas kernels, in_slabs(): pl.pallas_call(functools.partial(slab_kernel, sizes, (Q, nx, ny, nz, X //...  88.9 us
    unnamed x11, local copies, waits for them, and re-layouts  4.8 us

profile of v3, /device:TPU:0, one launch (start us, length us, event | category | flops | bytes accessed | tf_op | source)
XLA Modules:
  0.0 94.4 jit_solution(5451872980441396301)
XLA Ops:
  0.6 0.0 copy-start
  0.6 0.0 copy-start.1
  0.7 0.0 copy-start.2
  0.7 0.0 copy-start.3
  0.7 2.2 %copy.11 = f32[81,4,8,128]{3,0,2,1:T(8,128)S(1)} copy(f32[81,4,8,128]{3,2,1,0:T(8,128)} %param.5) | data formatting | bytes 2654208 | tf_op args[0]
  2.9 0.0 copy-done
  2.9 0.0 copy-done.1
  2.9 0.0 copy-done.2
  2.9 0.0 copy-done.3
  2.9 88.9 %shard_map.68 = (f32[4,8,81,128]{3,2,1,0:T(8,128)S(1)}, f32[4,8,81,128]{3,2,1,0:T(8,128)S(1)}) custom-call(f32[4,8,81,128]{3,2,1,0:T(8,128)S(1)} %bitcast.6, f32[32,32]{1,0:T(8,128)S(1)} %bitcast.9, bf16[648,648]{1,0:T(8,128)(2,1)S(1)} %copy-done, f32[81,81]{1,0:T(8,128)S(1)} %copy-done.2, f32[3,81,81]{2,1,0:T(8,128)S(1)} %copy-done.1), custom_call_target="tpu_custom_call" | custom-call | tf_op jit(solution)/shard_map/pallas_call | solution.py:973
  91.8 1.3 %copy.8 = f32[81,4,8,128]{3,2,1,0:T(8,128)} copy(f32[81,4,8,128]{3,0,2,1:T(8,128)S(1)} %bitcast.8) | data formatting | bytes 2654208
  93.1 1.3 %copy.9 = f32[81,4,8,128]{3,2,1,0:T(8,128)} copy(f32[81,4,8,128]{3,0,2,1:T(8,128)S(1)} %bitcast.7) | data formatting | bytes 2654208
Async XLA Ops:
  0.6 2.2 %copy-start = (bf16[648,648]{1,0:T(8,128)(2,1)S(1)}, bf16[648,648]{1,0:T(8,128)(2,1)}, u32[]{:S(2)}) copy-start(bf16[648,648]{1,0:T(8,128)(2,1)} %inverse_ref.1) | copy-start | bytes 2519428
  0.6 2.2 %copy-start.1 = (f32[3,81,81]{2,1,0:T(8,128)S(1)}, f32[3,81,81]{2,1,0:T(8,128)}, u32[]{:S(2)}) copy-start(f32[3,81,81]{2,1,0:T(8,128)} %f_ref.1) | copy-start | bytes 236200
  0.7 2.2 %copy-start.2 = (f32[81,81]{1,0:T(8,128)S(1)}, f32[81,81]{1,0:T(8,128)}, u32[]{:S(2)}) copy-start(f32[81,81]{1,0:T(8,128)} %m_ref.1) | copy-start | bytes 78736
  0.7 2.2 %copy-start.3 = (f32[4,8,32]{2,1,0:T(8,128)S(1)}, f32[4,8,32]{2,1,0:T(8,128)}, u32[]{:S(2)}) copy-start(f32[4,8,32]{2,1,0:T(8,128)} %param.6) | copy-start | bytes 12292

commit v4 on v3

--- a/solution.py
+++ b/solution.py
@@ -868,6 +868,12 @@
         return remote(out.at[h, where["gx"] * ny + where["gy"]], got.at[h, slab],
                       64 + (2 * kind + h) * G + o, where)
 
+    def piece_copy(o, n):
+        s, where = in_plane(o)
+        at = slice(0, A) if n == 0 else slice(A, M)
+        return remote(ores.at[1, where["gx"] * ny + where["gy"], at], rres.at[1, slab, at],
+                      96 + n * G + o, where)
+
     def send_out(ref, h, out, got, kind):
         for py in (0, 1):
             for r in range(0, A, 16):
@@ -877,6 +883,9 @@
                     v.append(ref[h, n // 2 + 1 - h, first:first + 16, :])
                 for n, x in enumerate(swap_source(v)):
                     out[h, n, py * A + r:py * A + r + 16, :] = x.astype(BF16)
+            if kind == 1 and h == 1 and py == 0:
+                for o in range(1, G):
+                    piece_copy(o, 0).start()
         v = []
         for n in range(G):
             t = ref[h, n // 2 + 1 - h, T:, :]
@@ -884,7 +893,10 @@
         for n, x in enumerate(swap_source(v)):
             out[h, n, 2 * A:, :] = x.astype(BF16)
         for o in range(1, G):
-            out_copy(out, got, h, kind, o).start()
+            if kind == 1 and h == 1:
+                piece_copy(o, 1).start()
+            else:
+                out_copy(out, got, h, kind, o).start()
         got[h, slab] = out[h, mine]
 
     def body(u, carry):
@@ -916,18 +928,20 @@
     finish(1, 0, 7, False, jnp.bool_(True))
     send_out(R, 1, ores, rres, 1)
 
-    def unpack(got, out):
+    def unpack(got, out, parts=(0, 1)):
         def merge(at):
             pairs = [swap([got[0, s, at, :].astype(F32), got[1, s, at, :].astype(F32)], 1, 2)
                      for s in range(G)]
             return [swap_slab([p[px] for p in pairs]) for px in (0, 1)]
 
-        for py in (0, 1):
+        for py in parts:
             for r in range(0, A, 16):
                 v = merge(slice(py * A + r, py * A + r + 16))
                 for px in (0, 1):
                     for (i, j), x in zip(cells, v[px]):
                         out[2 * i + px, 2 * j + py, r:r + 16, :] = x
+        if 1 not in parts:
+            return
         v = merge(slice(2 * A, M))
         for px in (0, 1):
             for (i, j), x in zip(cells, v[px]):
@@ -938,10 +952,12 @@
         for o in range(1, G):
             out_copy(osol, rsol, h, 0, o).wait()
     unpack(rsol, sol_ref)
-    for h in (0, 1):
+    for o in range(1, G):
+        out_copy(ores, rres, 0, 1, o).wait()
+    for n in (0, 1):
         for o in range(1, G):
-            out_copy(ores, rres, h, 1, o).wait()
-    unpack(rres, res_ref)
+            piece_copy(o, n).wait()
+        unpack(rres, res_ref, (n,))
 
 
 def in_slabs(sizes, right_side, cell_coef, cell_matrix, face_coupling, patch_inverse):
@@ -967,7 +983,7 @@
         V((D, 4 * LANES), F32), V((2 * D, 8 * Q), BF16),
         V((8, 2, *half), BF16), V((8, 2, *half), BF16), V((2, *half), BF16), V((2, *half), BF16),
         V(piece, BF16), V(piece, BF16), V(piece, BF16), V(piece, BF16),
-        pltpu.SemaphoreType.DMA((96,)), pltpu.SemaphoreType.DMA((96,)),
+        pltpu.SemaphoreType.DMA((112,)), pltpu.SemaphoreType.DMA((112,)),
     ]
     vmem = pl.BlockSpec(memory_space=pltpu.VMEM)
     sol, res = pl.pallas_call(

time: 94.5 us -> 93.2 us (0.986)
  Pallas kernels: 88.9 us -> 87.5 us
    pallas_call x1, Pallas kernels: 88.9 us -> 87.5 us  [in_slabs(): pl.pallas_call(functools.partial(slab_kernel, sizes, (Q, nx, ny, nz, X //...]
where the time goes in v4:
time: 93.2 us; the launch traced here: 93 us
  Pallas kernels  87.5 us (94%)
  local copies, waits for them, and re-layouts  4.8 us (5%)
    pallas_call x1, Pallas kernels, in_slabs(): pl.pallas_call(functools.partial(slab_kernel, sizes, (Q, nx, ny, nz, X //...  87.5 us
    unnamed x11, local copies, waits for them, and re-layouts  4.8 us

profile of v4, /device:TPU:0, one launch (start us, length us, event | category | flops | bytes accessed | tf_op | source)
XLA Modules:
  0.0 93.0 jit_solution(1062882651718487574)
XLA Ops:
  0.6 0.0 copy-start
  0.6 0.0 copy-start.1
  0.7 0.0 copy-start.2
  0.7 0.0 copy-start.3
  0.7 2.2 %copy.11 = f32[81,4,8,128]{3,0,2,1:T(8,128)S(1)} copy(f32[81,4,8,128]{3,2,1,0:T(8,128)} %param.5) | data formatting | bytes 2654208 | tf_op args[0]
  2.9 0.0 copy-done
  2.9 0.0 copy-done.1
  2.9 0.0 copy-done.2
  2.9 0.0 copy-done.3
  2.9 87.5 %shard_map.68 = (f32[4,8,81,128]{3,2,1,0:T(8,128)S(1)}, f32[4,8,81,128]{3,2,1,0:T(8,128)S(1)}) custom-call(f32[4,8,81,128]{3,2,1,0:T(8,128)S(1)} %bitcast.6, f32[32,32]{1,0:T(8,128)S(1)} %bitcast.9, bf16[648,648]{1,0:T(8,128)(2,1)S(1)} %copy-done, f32[81,81]{1,0:T(8,128)S(1)} %copy-done.2, f32[3,81,81]{2,1,0:T(8,128)S(1)} %copy-done.1), custom_call_target="tpu_custom_call" | custom-call | tf_op jit(solution)/shard_map/pallas_call | solution.py:989
  90.4 1.3 %copy.8 = f32[81,4,8,128]{3,2,1,0:T(8,128)} copy(f32[81,4,8,128]{3,0,2,1:T(8,128)S(1)} %bitcast.8) | data formatting | bytes 2654208
  91.7 1.3 %copy.9 = f32[81,4,8,128]{3,2,1,0:T(8,128)} copy(f32[81,4,8,128]{3,0,2,1:T(8,128)S(1)} %bitcast.7) | data formatting | bytes 2654208
Async XLA Ops:
  0.6 2.2 %copy-start = (bf16[648,648]{1,0:T(8,128)(2,1)S(1)}, bf16[648,648]{1,0:T(8,128)(2,1)}, u32[]{:S(2)}) copy-start(bf16[648,648]{1,0:T(8,128)(2,1)} %inverse_ref.1) | copy-start | bytes 2519428
  0.6 2.2 %copy-start.1 = (f32[3,81,81]{2,1,0:T(8,128)S(1)}, f32[3,81,81]{2,1,0:T(8,128)}, u32[]{:S(2)}) copy-start(f32[3,81,81]{2,1,0:T(8,128)} %f_ref.1) | copy-start | bytes 236200
  0.7 2.2 %copy-start.2 = (f32[81,81]{1,0:T(8,128)S(1)}, f32[81,81]{1,0:T(8,128)}, u32[]{:S(2)}) copy-start(f32[81,81]{1,0:T(8,128)} %m_ref.1) | copy-start | bytes 78736
  0.7 2.2 %copy-start.3 = (f32[4,8,32]{2,1,0:T(8,128)S(1)}, f32[4,8,32]{2,1,0:T(8,128)}, u32[]{:S(2)}) copy-start(f32[4,8,32]{2,1,0:T(8,128)} %param.6) | copy-start | bytes 12292
